TPU v7x, 8 devices: a whole 2x2x1 slice. The times are simulated.
8 devices in a mesh: dp: 8 (over z, y, x, core).
Axes of the slice: x: 2, y: 2, z: 1, core: 2. Of those that a mesh axis runs over, the one named last changes fastest.
Arguments:
- weights: float32 [12596224], P('dp')
- moment_one: float32 [12596224], P('dp')
- moment_two: float32 [12596224], P('dp')
- x_qkv: bfloat16 [32768, 1024], P('dp')
- dy_qkv: bfloat16 [32768, 3072], P('dp')
- x_proj: bfloat16 [32768, 1024], P('dp')
- dy_proj: bfloat16 [32768, 1024], P('dp')
- x_inter: bfloat16 [32768, 1024], P('dp')
- dy_inter: bfloat16 [32768, 4096], P('dp')
- x_out: bfloat16 [32768, 4096], P('dp')
- dy_out: bfloat16 [32768, 1024], P('dp')
- ln_grad: float32 [8, 4, 1024], P('dp')
Outputs:
- output 1: float32 [12596224], P('dp')
- output 2: float32 [12596224], P('dp')
- output 3: float32 [12596224], P('dp')
- output 4: bfloat16 [12596224], replicated
All inputs are finite; a program needn't handle non-finite values.
Results may differ from a plain program's by a relative error of at most 0.00574614.
Values sent between devices are 32-bit elements.
A program may use at most 1 GiB of HBM per device.

v0:
```python
import jax
import jax.numpy as jnp
from jax import lax
from jax.sharding import PartitionSpec as P

STEP = 10
LEARN_RATE = 0.5
BETA_ONE = 0.9
BETA_TWO = 0.999
EPSILON = 1e-6
DECAY = 0.01
NUM_SEGS = 13
CORR_ONE = 1.0 - BETA_ONE ** STEP
CORR_TWO = 1.0 - BETA_TWO ** STEP
CONTRACT_ROWS = (((0,), (0,)), ((), ()))


def tensor_sizes(layer_width):
    return [3 * layer_width * layer_width, 3 * layer_width, layer_width * layer_width, layer_width, layer_width, layer_width,
            4 * layer_width * layer_width, 4 * layer_width, 4 * layer_width * layer_width, layer_width, layer_width, layer_width]


def segment_index(positions, layer_width):
    seg_ids = jnp.zeros(positions.shape, jnp.int32)
    running_end = 0
    for tensor_size in tensor_sizes(layer_width):
        running_end = running_end + tensor_size
        seg_ids = seg_ids + (positions >= running_end).astype(jnp.int32)
    return seg_ids


def tensor_sums(values, seg_ids):
    seg_range = jnp.arange(NUM_SEGS, dtype=jnp.int32)[:, None]
    return jnp.sum(jnp.where(seg_ids[None, :] == seg_range, values[None, :], 0.0), axis=1)


def per_element(table, seg_ids):
    seg_range = jnp.arange(NUM_SEGS, dtype=jnp.int32)[:, None]
    return jnp.sum(jnp.where(seg_ids[None, :] == seg_range, table[:, None], 0.0), axis=0)


def weight_grad(x_rows, dy_rows):
    return lax.dot_general(x_rows, dy_rows, CONTRACT_ROWS, preferred_element_type=jnp.float32)


def bias_grad(dy_rows):
    return jnp.sum(dy_rows, axis=0, dtype=jnp.float32)


def flat_grad(act_pairs, ln_rows, total_len):
    x_qkv, dy_qkv, x_proj, dy_proj, x_inter, dy_inter, x_out, dy_out = act_pairs
    pieces = [weight_grad(x_qkv, dy_qkv), bias_grad(dy_qkv), weight_grad(x_proj, dy_proj), bias_grad(dy_proj),
              ln_rows[0], ln_rows[1], weight_grad(x_inter, dy_inter), bias_grad(dy_inter),
              weight_grad(x_out, dy_out), bias_grad(dy_out), ln_rows[2], ln_rows[3]]
    filled_len = sum(grad_piece.size for grad_piece in pieces)
    pieces.append(jnp.zeros((total_len - filled_len,), jnp.float32))
    return jnp.concatenate([grad_piece.reshape(-1) for grad_piece in pieces])


def adam_direction(grad_hat, weights, moment_one, moment_two, seg_ids):
    new_m = BETA_ONE * moment_one + (1.0 - BETA_ONE) * grad_hat
    new_v = BETA_TWO * moment_two + (1.0 - BETA_TWO) * grad_hat * grad_hat
    decay_mask = ((seg_ids == 0) | (seg_ids == 2) | (seg_ids == 6) | (seg_ids == 8)).astype(jnp.float32)
    update = (new_m / CORR_ONE) / (jnp.sqrt(new_v / CORR_TWO) + EPSILON) + DECAY * decay_mask * weights
    return new_m, new_v, update


def trust_ratio(w_sq, u_sq):
    w_norm = jnp.sqrt(w_sq)
    u_norm = jnp.sqrt(u_sq)
    both_pos = (w_norm > 0) & (u_norm > 0)
    return jnp.where(both_pos, w_norm / jnp.where(u_norm > 0, u_norm, 1.0), 1.0)


def solution(mesh):
    axis_size = mesh.shape['dp']

    def local_step(weights, moment_one, moment_two, x_qkv, dy_qkv, x_proj, dy_proj, x_inter, dy_inter, x_out, dy_out, ln_grad):
        layer_width = x_qkv.shape[1]
        shard_len = weights.shape[0]
        act_pairs = (x_qkv, dy_qkv, x_proj, dy_proj, x_inter, dy_inter, x_out, dy_out)
        local_grad = flat_grad(act_pairs, ln_grad[0], shard_len * axis_size)
        mean_grad = lax.psum_scatter(local_grad, 'dp', scatter_dimension=0, tiled=True) / axis_size
        grad_norm = jnp.sqrt(lax.psum(jnp.sum(mean_grad * mean_grad), 'dp'))
        grad_hat = mean_grad / jnp.maximum(1.0, grad_norm)
        positions = lax.axis_index('dp') * shard_len + lax.iota(jnp.int32, shard_len)
        seg_ids = segment_index(positions, layer_width)
        new_m, new_v, update = adam_direction(grad_hat, weights, moment_one, moment_two, seg_ids)
        part_sums = jnp.stack([tensor_sums(weights * weights, seg_ids), tensor_sums(update * update, seg_ids)])
        total_sums = lax.psum(part_sums, 'dp')
        trust_vec = trust_ratio(total_sums[0], total_sums[1])
        new_w = weights - LEARN_RATE * per_element(trust_vec, seg_ids) * update
        full_w = lax.optimization_barrier(lax.all_gather(new_w, 'dp', axis=0, tiled=True))
        params = full_w.astype(jnp.bfloat16)
        return new_w, new_m, new_v, params

    row_spec = P('dp', None)
    in_specs = (P('dp'), P('dp'), P('dp'), row_spec, row_spec, row_spec, row_spec, row_spec, row_spec, row_spec, row_spec, P('dp', None, None))
    out_specs = (P('dp'), P('dp'), P('dp'), P())
    return jax.shard_map(local_step, mesh=mesh, in_specs=in_specs, out_specs=out_specs, check_vma=False)
```

profile of v0, /device:TPU:0, one launch (start us, length us, event | category | flops | bytes accessed | tf_op | source)
XLA Modules:
  0.0 1350.0 jit_solution(15841941200187458773)
XLA Ops:
  7.2 0.0 all-reduce.3.cloned.1.call-start
  7.2 1.5 fusion.18
  8.7 11.5 convert_reduce_fusion.1
  20.2 4.2 copy-done.1
  24.4 30.4 %convolution_bitcast_fusion.2 = f32[128,24,8,128]{3,2,1,0:T(8,128)} fusion(bf16[4096,1024]{1,0:T(8,128)(2,1)} %param.15, bf16[4096,3072]{1,0:T(8,128)(2,1)S(1)} %copy-done.1), kind=kOutput, calls=%fused_computation.32 | convolution fusion | flops 25769803776 | bytes 46137344 | tf_op jit(solution)/shard_map/dot_general | solution.py:43
  54.8 12.3 copy.16
  67.1 10.1 constant_dynamic-update-slice_fusion.11
  77.2 0.0 slice-done
  77.2 1.3 convert_reduce_fusion.3
  78.4 11.6 convolution_bitcast_fusion.3
  90.0 0.0 slice-start.2
  90.0 3.0 copy.17
  93.1 11.8 convert_reduce_fusion
  104.9 0.0 slice-done.2
  104.9 0.3 slice-done.3
  105.1 42.3 %convolution_bitcast_fusion.1 = f32[128,32,8,128]{3,2,1,0:T(8,128)} fusion(bf16[4096,1024]{1,0:T(8,128)(2,1)S(1)} %bitcast.45, bf16[4096,4096]{1,0:T(8,128)(2,1)} %param.20), kind=kOutput, calls=%fused_computation.10 | convolution fusion | flops 34359738368 | bytes 58720256 | tf_op jit(solution)/shard_map/dot_general | solution.py:43
  147.5 9.4 copy.18
  156.9 4.6 convert_reduce_fusion.2
  161.5 43.8 %convolution_bitcast_fusion = f32[512,8,8,128]{3,2,1,0:T(8,128)} fusion(bf16[4096,4096]{1,0:T(8,128)(2,1)} %param.21, bf16[4096,1024]{1,0:T(8,128)(2,1)} %param.22), kind=kOutput, calls=%fused_computation.9 | convolution fusion | flops 34359738368 | bytes 58720256 | tf_op jit(solution)/shard_map/dot_general | solution.py:43
  205.3 9.4 copy.19
  214.7 0.6 constant_dynamic-update-slice_fusion.10
  215.3 4.4 constant_dynamic-update-slice_fusion.9
  219.7 0.6 constant_dynamic-update-slice_fusion.8
  220.3 0.6 constant_dynamic-update-slice_fusion.7
  220.9 0.6 constant_dynamic-update-slice_fusion.6
  221.5 6.1 constant_dynamic-update-slice_fusion.5
  227.6 0.6 constant_dynamic-update-slice_fusion.4
  228.2 6.1 constant_dynamic-update-slice_fusion.3
  234.3 0.6 constant_dynamic-update-slice_fusion.2
  234.9 0.6 constant_dynamic-update-slice_fusion.1
  235.4 0.6 constant_dynamic-update-slice_fusion
  236.0 0.0 all-reduce.3.cloned.1.call-update
  236.1 0.0 all-gather.3.cloned.1.call-start
  236.1 570.2 %all-reduce.3.cloned.1.call-done = f32[12596224]{0:T(1024)} async-done(((f32[12596224]{0:T(1024)}), f32[12596224]{0:T(1024)}) %all-reduce.3.cloned.1.call-update) | async-done | bytes 50384912
  806.4 4.5 multiply_reduce_fusion
  810.9 8.8 convert_add_fusion
  819.7 22.4 %psum.14 = f32[]{:T(128)} all-reduce(f32[]{:T(128)} %multiply_reduce_fusion), channel_id=1, replica_groups=mesh['dp'=8] {'dp'}, use_global_device_ids=true, to_apply=%region_7.8 | all-reduce | flops 1 | bytes 8 | tf_op jit(solution)/shard_map/psum | solution.py:84
  842.9 24.1 %fusion.16 = (f32[1574528]{0:T(1024)}, f32[1574528]{0:T(1024)}, f32[1574528]{0:T(1024)}, f32[1574528]{0:T(1024)}) fusion(f32[1574528]{0:T(1024)} %param.12, s32[]{:T(128)S(6)} %mul.57, f32[]{:T(128)S(6)} %max.3, f32[12596224]{0:T(1024)} %all-reduce.3.cloned.1.call-done, u32[]{:T(128)S(6)} %multiply.4, f32[1574528]{0:T(1024)} %param.13, f32[1574528]{0:T(1024)} %param.14), kind=kLoop, calls=%fused_computation.51 | loop fusion | flops 96046208 | bytes 50384908 | tf_op jit(solution)/shard_map/mul | solution.py:89
  867.0 56.1 %select_reduce_fusion.2 = (f32[13]{0:T(128)S(1)}, f32[13]{0:T(128)S(1)}) fusion(f32[1574528]{0:T(1024)} %get-tuple-element.9, s32[1574528]{0:T(1024)} %convert_add_fusion, f32[1574528]{0:T(1024)} %get-tuple-element.6), kind=kLoop, calls=%fused_computation.2 | loop fusion | flops 102344288 | bytes 18894440 | tf_op jit(solution)/shard_map/reduce_sum | solution.py:34
  923.1 24.4 %psum.15 = f32[2,13]{1,0:T(2,128)S(1)} all-reduce(f32[2,13]{1,0:T(2,128)S(1)} %pad_maximum_fusion), channel_id=1, replica_groups=mesh['dp'=8] {'dp'}, use_global_device_ids=true, to_apply=%region_9.10 | all-reduce | flops 26 | bytes 208 | tf_op jit(solution)/shard_map/psum | solution.py:90
  947.5 93.5 %select_reduce_fusion = f32[1574528]{0:T(1024)} fusion(f32[13]{0:T(128)S(1)} %fusion.14, s32[1574528]{0:T(1024)} %convert_add_fusion), kind=kLoop, calls=%fused_computation | loop fusion | flops 59832064 | bytes 12596276 | tf_op jit(solution)/shard_map/reduce_sum | solution.py:39
  1041.0 15.5 %multiply_subtract_fusion = f32[1574528]{0:T(1024)S(1)} fusion(f32[1574528]{0:T(1024)} %param.12, f32[1574528]{0:T(1024)} %select_reduce_fusion, s32[]{:T(128)S(6)} %mul.57, f32[1574528]{0:T(1024)} %get-tuple-element.8, f32[1574528]{0:T(1024)} %get-tuple-element.7), kind=kLoop, calls=%fused_computation.13 | loop fusion | flops 83449984 | bytes 31490564 | tf_op jit(solution)/shard_map/sub | solution.py:92
  1056.5 0.0 copy-start
  1056.6 2.7 copy-done
  1059.3 30.2 %reshape.91 = f32[1,1,1574528]{2,1,0:T(1,128)} reshape(f32[1574528]{0:T(1024)S(1)} %multiply_subtract_fusion) | data formatting | bytes 12596224
  1089.5 0.0 all-gather.3.cloned.1.call-update
  1089.5 227.8 %all-gather.3.cloned.1.call-done = f32[8,1,1574528]{2,1,0:T(1,128)} async-done(((f32[1,1,1574528]{2,1,0:T(1,128)}), f32[8,1,1574528]{2,1,0:T(1,128)}) %all-gather.3.cloned.1.call-update) | async-done | bytes 50384912 | tf_op jit(solution)/shard_map/all_gather | solution.py:93
  1317.3 25.4 %convert_element_type.116 = bf16[12596224]{0:T(1024)(128)(2,1)} convert(f32[12596224]{0:T(1024)} %bitcast.33) | non-fusion elementwise | flops 12596224 | bytes 75577344 | tf_op jit(solution)/shard_map/convert_element_type | solution.py:94
  (19 shorter events, 0.1 us)
Async XLA Ops:
  7.2 799.2 %all-reduce.3.cloned.1.call-start = ((), (), s32[]{:S(2)}) async-start(), calls=%async_computation.1 | async-start | bytes 100769792
  8.7 15.7 %copy-start.1 = (bf16[4096,3072]{1,0:T(8,128)(2,1)S(1)}, bf16[4096,3072]{1,0:T(8,128)(2,1)}, u32[]{:S(2)}) copy-start(bf16[4096,3072]{1,0:T(8,128)(2,1)} %param.16) | copy-start | bytes 75497472
  54.8 22.4 %slice-start = ((s8[8388608]{0:T(1024)(128)(4,1)}), s8[4194304]{0:T(1024)(128)(4,1)S(1)}, s32[]{:S(2)}) async-start(s8[8388608]{0:T(1024)(128)(4,1)} %bitcast.36), calls=%async_computation.2 | async-start | bytes 8388608
  67.1 10.1 slice-start.1
  90.0 14.9 %slice-start.2 = ((s8[8388608]{0:T(1024)(128)(4,1)}), s8[4194304]{0:T(1024)(128)(4,1)S(1)}, s32[]{:S(2)}) async-start(s8[8388608]{0:T(1024)(128)(4,1)} %bitcast.44), calls=%async_computation.4 | async-start | bytes 8388608
  93.1 12.1 slice-start.3
  205.3 9.4 copy-start.2
  214.7 5.6 copy-start.6
  214.7 6.2 copy-start.5
  228.2 6.7 copy-start.4
  228.2 7.3 copy-start.3
  236.1 1081.2 %all-gather.3.cloned.1.call-start = ((), (), s32[]{:S(2)}) async-start(), calls=%async_computation | async-start | bytes 56683008 | tf_op jit(solution)/shard_map/all_gather | solution.py:93
  1056.5 2.7 copy-start
Sparse Core Ops, SparseCore 0:
  236.2 570.1 all-reduce.2
  1089.6 227.6 all-gather.2
where the time goes:
time: 1360 us; the launch traced here: 1350 us
  waiting for transfers between devices  798 us (59%)
  other arithmetic  257 us (19%)
  matrix products  128 us (9%)
  local copies, waits for them, and re-layouts  104 us (8%)
  blocking collectives  46.8 us (3%)
  between operations  15.3 us (1%)
    unnamed x3, waiting for transfers between devices  570 us
    all_gather x1, waiting for transfers between devices, local_step(): lax.all_gather(new_w, 'dp', axis=0, tiled=True)  228 us
    dot_general x4, matrix products, weight_grad(): lax.dot_general(x_rows, dy_rows, CONTRACT_ROWS, preferred_element_type=jn...  128 us
    unnamed x38, local copies, waits for them, and re-layouts  102 us
    reduce_sum x1, other arithmetic, per_element(): jnp.sum(jnp.where(seg_ids[None, :] == seg_range, table[:, None], 0.0), ax...  93.5 us
    reduce_sum x1, other arithmetic, tensor_sums(): jnp.sum(jnp.where(seg_ids[None, :] == seg_range, values[None, :], 0.0), a...  56.1 us
    reduce_sum x4, other arithmetic, bias_grad(): return jnp.sum(dy_rows, axis=0, dtype=jnp.float32)  29.1 us
  transfers between devices with their start and end apart: 2, of which 2 were waited for; matrix products, arithmetic and copies ran while one was open for 0% of the time, Pallas kernels for 0%

commit v1 on v0

v1 whole, which is shorter than its diff:
```python
import jax
import jax.numpy as jnp
from jax import lax
from jax.experimental import pallas as pl
from jax.experimental.pallas import tpu as pltpu
from jax.sharding import PartitionSpec as P

STEP = 10
LEARN_RATE = 0.5
BETA_ONE = 0.9
BETA_TWO = 0.999
EPSILON = 1e-6
DECAY = 0.01
CORR_ONE = 1.0 - BETA_ONE ** STEP
CORR_TWO = 1.0 - BETA_TWO ** STEP

D = 1024
N_DEV = 8
TOKENS = 4096
LANES = 128
SHARD_ROWS = 12301
TOTAL_ROWS = N_DEV * SHARD_ROWS
KC = 1024
CHUNKS = TOKENS // KC
BLOCK = 512
TASKS = 24
STEPS = TASKS * CHUNKS
UR = 128
UNITS = 12
HALF = UNITS // 2
F32 = jnp.float32
BF16 = jnp.bfloat16
MIB = 1024 * 1024

SIZES = [24576, 24, 8192, 8, 8, 8, 32768, 32, 32768, 8, 8, 8]
STARTS = [sum(SIZES[:pos]) for pos in range(len(SIZES) + 1)]
SHARE = UNITS * D
NOMINAL = [0, 12288, 24600, 36912, 49200, 61488, 73808, 86096]
FIRST_TENSOR = [max(t for t, at in enumerate(STARTS[:-1]) if at <= SHARD_ROWS * dev) for dev in range(N_DEV)]
PAST_TENSOR = [1 + max(t for t, at in enumerate(STARTS[:-1]) if at < SHARD_ROWS * (dev + 1)) for dev in range(N_DEV)]
EDGE = 48
WIN = 12416
UP, DOWN = 24, 16
FEW = [0, 1, 5, 6, 7, 11]
MANY = [0, 3, 3, 6, 9, 9]
WIDE = [0, 0, 1, 2, 0, 3]
B1, Y1, X1 = range(1, 4)


def pick(index, values):
    out = jnp.int32(values[-1])
    for pos in reversed(range(len(values) - 1)):
        out = jnp.where(index == pos, jnp.int32(values[pos]), out)
    return out


def tile(index, size):
    return pl.ds(pl.multiple_of(index * size, size), size)


def each(lo, hi, body):
    def step(pos, carry):
        body(pos)
        return carry
    lax.fori_loop(lo, hi, step, lo)


def other(bit):
    return 1 - bit


def device(y, x, core):
    return 4 * y + 2 * x + core


def neighbours():
    me = lax.axis_index('dp')
    chip, core = me // 2, me % 2
    x, y = chip % 2, chip // 2
    return me, chip, core, device(y, x, other(core)), device(y, other(x), core), device(other(y), x, core)


def local(src, dst, sem):
    return pltpu.make_async_copy(src, dst, sem)


def remote(src, dst, send_sem, recv_sem, dev):
    return pltpu.make_async_remote_copy(src_ref=src, dst_ref=dst, send_sem=send_sem, recv_sem=recv_sem,
                                        device_id=(dev,), device_id_type=pl.DeviceIdType.MESH)


def act_on(copy, act):
    if act == 'start':
        copy.start()
    elif act == 'sent':
        copy.wait_send()
    else:
        copy.wait()


def enter(devices):
    barrier = pltpu.get_barrier_semaphore()
    for dev in devices:
        pl.semaphore_signal(barrier, inc=1, device_id=(dev,), device_id_type=pl.DeviceIdType.MESH)
    pl.semaphore_wait(barrier, len(devices))


def task_of(n):
    six = HALF
    mid = n - six
    first, last = n < six, n >= 3 * six
    t = jnp.where(first, 0, jnp.where(last, X1, B1 + mid % 2))
    i = jnp.where(first, n, jnp.where(last, n - 3 * six, mid // 2))
    return t, i


def chip_of(t, chip):
    x, y = chip % 2, chip // 2
    return 2 * ((y + other(t % 2)) % 2) + (x + other(t // 2)) % 2


def is_square(i):
    return i % 3 == 1


def is_edge(q):
    return q % 3 == 0


def operands_of(q, i):
    square, odd, pair = is_square(i), i % 2, i // 2
    kind = jnp.where(is_edge(q), q, jnp.where(square, 2 * q - 1, 2))
    rb = jnp.where(q == 0, odd, jnp.where(is_edge(q), 2 + 3 * odd + pair, jnp.where(square, i // 4, q - 1)))
    cb = jnp.where(q == 0, pair, jnp.where(is_edge(q) | square, 0, pick(i, WIDE)))
    return kind, rb, cb


def units_of(q, i, par):
    square = is_square(i)
    few = q - 1 == par
    cnt = jnp.where(few, jnp.where(square, 4, 1), jnp.where(square, 0, 3))
    s0 = jnp.where(square | (par == 0), 0, 2 * q - 1)
    u0 = jnp.where(few, pick(i, FEW), pick(i, MANY))
    edge = is_edge(q)
    return (jnp.where(edge, 0, s0), jnp.where(edge, jnp.where(i % 2 == par, 4, 0), cnt),
            jnp.where(edge, 4 * (i // 2), u0))


def bias_of(q, i):
    square = is_square(i)
    need = jnp.where(is_edge(q), jnp.where(q == 0, i % 2, i) == 0, jnp.where(q == 1, i == 1, ~square))
    return need, jnp.where(q == 0, i // 2, jnp.where(q == 2, pick(i, WIDE), 0))


def reduce_kernel(xq, dyq, xp, dyp, xi, dyi, xo, dyo, ln,
                  g_a, g_b, g_c, v_out, ss_out, sib_land, x_land, y_land,
                  xbuf, dybuf, acc, part, stage, stage_r, flat, vec, vsum, vflat, vland, lnbuf, ss, ss_small,
                  x_sem, dy_sem, sib_send, sib_recv, out_send, x_recv, y_recv,
                  v_send, v_recv, st_sem, sr_sem, fl_sem, misc_sem):
    me, chip, core, sib, xn, yn = neighbours()
    kinds = ((xq, dyq), (xp, dyp), (xi, dyi), (xo, dyo))
    here = X1

    def arrived(ref, sem):
        remote(ref, ref, misc_sem.at[0], sem, sib).wait_recv()

    def issue(j):
        n, slot = j // CHUNKS, j % CHUNKS
        t, i = task_of(n)
        kind, rb, cb = operands_of(chip_of(t, chip), i)
        for which, (x_ref, dy_ref) in enumerate(kinds):
            @pl.when(kind == which)
            def _():
                local(x_ref.at[tile(slot, KC), tile(rb, BLOCK)], xbuf.at[slot], x_sem.at[slot]).start()
                local(dy_ref.at[tile(slot, KC), tile(cb, D)], dybuf.at[slot], dy_sem.at[slot]).start()

    for j in range(CHUNKS - 1):
        issue(jnp.int32(j))
    ln_copy = local(ln, lnbuf, misc_sem.at[0])
    ln_copy.start()
    enter((sib, xn, yn))
    ln_copy.wait()
    ss[...] = jnp.zeros_like(ss)
    vec[...] = jnp.zeros_like(vec)
    for t in range(4):
        for q in (1, 3):
            @pl.when(chip_of(jnp.int32(t), chip) == q)
            def _():
                vec[t, 1:3, :] = lnbuf[q - 1:q + 1, :]

    def own_units(n, par, body):
        t, i = task_of(n)
        s0, cnt, u0 = units_of(chip_of(t, chip), i, par)
        each(s0, s0 + cnt, lambda s: body(t, u0 + s - s0, s, t * UNITS + u0 + s - s0))

    def relayed(t, u, do):
        @pl.when((t == B1) & (u % 2 == 1))
        def _():
            do(y_land, y_recv)

        @pl.when((t == Y1) & (u % 2 == 0))
        def _():
            do(x_land, x_recv)

    def prefetch(n):
        def body(t, u, s, e):
            arrived(sib_land.at[e], sib_recv.at[e])
            local(sib_land.at[e], stage.at[s], st_sem.at[s]).start()

            def more(land, recv):
                arrived(land.at[u // 2], recv.at[u // 2])
                local(land.at[u // 2], stage_r.at[s], sr_sem.at[s]).start()
            relayed(t, u, more)
        own_units(n, core, body)

    def combine(n):
        def body(t, u, s, e):
            local(sib_land.at[e], stage.at[s], st_sem.at[s]).wait()
            part[e] = acc[n % 3, tile(s, UR), :] + stage[s]

            def more(land, recv):
                local(land.at[u // 2], stage_r.at[s], sr_sem.at[s]).wait()
                part[e] = part[e] + stage_r[s]
            relayed(t, u, more)
        own_units(n, core, body)
        t, i = task_of(n)

        @pl.when(i == HALF - 1)
        def _():
            remote(vec.at[t], vland.at[t], v_send.at[t], v_recv.at[t], sib).wait()
            vsum[t] = vec[t] + vland[t]

            @pl.when(t == Y1)
            def _():
                arrived(vland.at[4], v_recv.at[4])
                vsum[t] = vsum[t] + vland[4]

    def send_own(n):
        def body(t, u, s, e):
            def go(land, recv, slot, dev):
                remote(part.at[e], land.at[slot], out_send.at[e], recv.at[slot], dev).start()

            @pl.when((t == 0) & (u % 2 == 0))
            def _():
                go(x_land, x_recv, u // 2, xn)

            @pl.when((t == 0) & (u % 2 == 1))
            def _():
                go(y_land, y_recv, u // 2, yn)

            @pl.when(t == B1)
            def _():
                go(x_land, x_recv, HALF + u, xn)

            @pl.when(t == Y1)
            def _():
                go(y_land, y_recv, HALF + u, yn)
        own_units(n, core, body)
        t, i = task_of(n)
        for way, dev in enumerate((xn, xn, yn)):
            @pl.when((i == HALF - 1) & (t == way))
            def _():
                remote(vsum.at[t], vland.at[4 + way], v_send.at[4 + way], v_recv.at[4 + way], dev).start()

    def sib_units(n, act):
        def body(t, u, s, e):
            act_on(remote(acc.at[n % 3, tile(s, UR)], sib_land.at[e], sib_send.at[e], sib_recv.at[e], sib), act)
        own_units(n, other(core), body)

    def task(n):
        t, i = task_of(n)
        need, row = bias_of(chip_of(t, chip), i)
        a = n % 3

        @pl.when(n >= 3)
        def _():
            sib_units(n - 3, 'sent')

        def chunk(slot):
            j = n * CHUNKS + slot

            @pl.when(j + CHUNKS - 1 < STEPS)
            def _():
                issue(j + CHUNKS - 1)
            local(xq.at[tile(0, KC), tile(0, BLOCK)], xbuf.at[slot], x_sem.at[slot]).wait()
            local(dyq.at[tile(0, KC), tile(0, D)], dybuf.at[slot], dy_sem.at[slot]).wait()

            def dot():
                return lax.dot_general(xbuf[slot], dybuf[slot], (((0,), (0,)), ((), ())),
                                       preferred_element_type=F32)

            @pl.when(slot == 0)
            def _():
                acc[a] = dot()

            @pl.when(slot > 0)
            def _():
                acc[a] += dot()

            @pl.when(need)
            def _():
                def add(r, total):
                    block = dybuf[slot, tile(r, LANES), :].astype(F32)
                    return total + jnp.sum(block.reshape(-1, 8, D), axis=0)
                total = lax.fori_loop(0, KC // LANES, add, jnp.zeros_like(ss))
                vec[t, pl.ds(row, 1), :] += jnp.sum(total, axis=0, keepdims=True)

            @pl.when((slot == 1) & (n > 0))
            def _():
                prefetch(n - 1)

            @pl.when((slot == 2) & (n > 0))
            def _():
                combine(n - 1)
                send_own(n - 1)
        each(0, CHUNKS, chunk)
        sib_units(n, 'start')

        @pl.when(i == HALF - 1)
        def _():
            remote(vec.at[t], vland.at[t], v_send.at[t], v_recv.at[t], sib).start()

    each(0, TASKS, task)
    prefetch(jnp.int32(TASKS - 1))
    combine(jnp.int32(TASKS - 1))
    each(TASKS - 3, TASKS, lambda n: sib_units(n, 'sent'))

    few = chip - 1 == core
    mid = jnp.logical_not(is_edge(chip))
    past = chip == 2

    def write_unit(u, slot):
        def go(dst):
            local(flat.at[slot], dst, fl_sem.at[slot]).start()

        @pl.when(chip == 0)
        def _():
            go(g_a.at[tile(u % 4, UR), tile(u // 4, 8)])

        @pl.when(chip == 3)
        def _():
            go(g_c.at[tile(u, UR)])
        square = jnp.where((u >= FEW[1]) & (u < FEW[2]), u - FEW[1],
                           jnp.where((u >= FEW[4]) & (u < FEW[-1]), u - 3, -1))
        col = jnp.where(u < FEW[2], 0, jnp.where(u < FEW[4], u - 4, 3))

        @pl.when(mid & few & (square < 0))
        def _():
            go(g_b.at[tile(jnp.where(past, 0, 2), UR), tile(col, 8)])

        @pl.when(mid & few & (square >= 0))
        def _():
            go(g_c.at[tile(jnp.where(past, 4, 0) + square, UR)])

        @pl.when(mid & jnp.logical_not(few))
        def _():
            go(g_b.at[tile(u % 3, UR), tile(u // 3, 8)])

    def written(slot):
        local(flat.at[slot], g_c.at[tile(0, UR)], fl_sem.at[slot]).wait()

    def finish(u):
        copies = []
        for e, (land, recv) in enumerate(((x_land, x_recv), (y_land, y_recv))):
            arrived(land.at[HALF + u], recv.at[HALF + u])
            copies.append(local(land.at[HALF + u], stage.at[e], st_sem.at[e]))
            copies[e].start()
        slot = u % 2

        @pl.when(u >= 2)
        def _():
            written(slot)
        for c in copies:
            c.wait()

        def add(r, total):
            rows = tile(r, 16)
            val = part[here * UNITS + u, rows, :] + stage[0, rows, :] + stage[1, rows, :]
            flat[slot, rows] = val.reshape(16, 8, LANES)
            return total + val[0:8] * val[0:8] + val[8:16] * val[8:16]
        ss[...] += lax.fori_loop(0, UR // 16, add, jnp.zeros_like(ss))
        write_unit(u, slot)

    each(0, UNITS, finish)
    arrived(vland.at[5], v_recv.at[5])
    arrived(vland.at[6], v_recv.at[6])
    val = vsum[here] + vland[5] + vland[6]
    vflat[...] = val.reshape(8, 8, LANES)
    total = ss[...] + jnp.where(core == 0, 1.0, 0.0).astype(F32) * (val * val)
    ss_small[...] = sum(total[:, LANES * c:LANES * (c + 1)] for c in range(8))
    tail = [local(vflat, v_out, misc_sem.at[0]), local(ss_small, ss_out, misc_sem.at[1])]
    for c in tail:
        c.start()
    written(0)
    written(1)
    for c in tail:
        c.wait()
    each(0, here * UNITS, lambda e: remote(part.at[e], x_land.at[0], out_send.at[e], x_recv.at[0], xn).wait_send())
    for way in range(3):
        remote(vsum.at[way], vland.at[4], v_send.at[4 + way], v_recv.at[4], xn).wait_send()


def shape(*dims, dtype=F32):
    return jax.ShapeDtypeStruct(dims, dtype)


def vmem(*dims, dtype=F32):
    return pltpu.VMEM(dims, dtype)


def dmas(*counts):
    return [pltpu.SemaphoreType.DMA(c if isinstance(c, tuple) else (c,)) for c in counts]


def any_space(count):
    return [pl.BlockSpec(memory_space=pltpu.HBM)] * count


def params_of(collective_id, mib):
    return pltpu.CompilerParams(collective_id=collective_id, has_side_effects=True, vmem_limit_bytes=mib * MIB)


def reduce_call(acts, ln_rows):
    lands = UNITS + HALF
    outs = [shape(512, 24, LANES), shape(384, 32, LANES), shape(1536, 8, LANES), shape(8, 8, LANES), shape(8, LANES),
            shape(4 * UNITS, UR, D), shape(lands, UR, D), shape(lands, UR, D)]
    return pl.pallas_call(
        reduce_kernel,
        out_shape=outs,
        in_specs=any_space(len(acts) + 1),
        out_specs=any_space(len(outs)),
        scratch_shapes=[
            vmem(CHUNKS, KC, BLOCK, dtype=BF16), vmem(CHUNKS, KC, D, dtype=BF16), vmem(3, BLOCK, D),
            vmem(4 * UNITS, UR, D), vmem(4, UR, D), vmem(4, UR, D), vmem(2, UR, 8, LANES),
            vmem(4, 8, D), vmem(4, 8, D), vmem(8, 8, LANES), vmem(7, 8, D), vmem(4, D), vmem(8, D), vmem(8, LANES),
            *dmas(CHUNKS, CHUNKS, 4 * UNITS, 4 * UNITS, 3 * UNITS, lands, lands, 7, 7, 4, 4, 2, 2)],
        compiler_params=params_of(0, 62),
        name='grad_reduce',
    )(*acts, ln_rows)


PARTS = 16
SEG = SHARE // PARTS
CUTS = [SEG * j for j in range(PARTS)] + [SHARD_ROWS]
BLK = 64
FULL = SHARE // BLK
LOADS = 8
LOAD = SHARE // LOADS
GB = FULL // LOADS


def update_kernel(w_in, m_in, v_in, ga, gb, gc, vg, ss_in,
                  wbuf, mbuf, vbuf, params, full,
                  gbuf, cin, ssl, sums, rates,
                  load_sem, g_sem, edge_send, edge_recv, ss_send, ss_recv, sum_send, sum_recv,
                  own_send, own_copy, x_recv, y_recv, d_recv, s_recv, fwd_send, sib_fwd, cin_sem):
    me, chip, core, sib, xn, yn = neighbours()

    def floor_of(dev):
        return DOWN * (SHARD_ROWS * dev // DOWN)

    def in_window(dev, row):
        return row - SHARD_ROWS * dev + EDGE

    def load_rows(k):
        return pl.ds(LOAD * k, LOAD if k < LOADS - 1 else SHARD_ROWS - LOAD * k)

    loads = [[local(src.at[load_rows(k)], dst.at[load_rows(k)], load_sem.at[e, k])
              for e, (src, dst) in enumerate(((w_in, wbuf), (m_in, mbuf), (v_in, vbuf)))] for k in range(LOADS)]

    def when_in(lo, hi, do, *args):
        @pl.when((me >= lo) & (me <= hi))
        def _():
            do(*args)

    def g_loads(act):
        start = in_window(me, pick(me, NOMINAL))

        def go(*copies):
            for e, (src, lo, size, at) in enumerate(copies):
                act_on(local(src.at[pl.ds(lo, size)], gbuf.at[pl.ds(start + at, size)], g_sem.at[e]), act)
        two, one = SIZES[2], SHARE - SIZES[2]
        tail = (vg, 0, UP, SHARE)
        when_in(0, 0, go, (ga, 0, SHARE, 0))
        when_in(1, 1, go, (ga, 0, SHARE, 0), tail)
        when_in(2, 2, go, (gc, 0, two, 0), (vg, 0, UP, two), (gb, two, one, two + UP))
        when_in(3, 4, go, (gb, 0, SHARE, 0))
        when_in(5, 5, go, (gb, 0, one, 0), (vg, 0, SIZES[7], one), (gc, one, two, one + SIZES[7]))
        when_in(6, 6, go, (gc, 0, SHARE, 0))
        when_in(7, 7, go, (gc, 0, SHARE, 0), tail)

    ss_copy = local(ss_in, ssl.at[me], cin_sem.at[0])
    ss_copy.start()
    g_loads('start')
    for group in loads:
        for c in group:
            c.start()
    sums[...] = jnp.zeros_like(sums)
    ss_copy.wait()
    others = [lax.rem(me + e, N_DEV) for e in range(1, N_DEV)]
    enter(others)

    def share(buf, send, recv, act):
        for e, dev in enumerate(others):
            if act == 'get':
                remote(buf.at[dev], buf.at[dev], send.at[e], recv.at[dev], dev).wait_recv()
            else:
                act_on(remote(buf.at[me], buf.at[me], send.at[e], recv.at[me], dev), act)

    share(ssl, ss_send, ss_recv, 'start')

    def edges(act):
        def go(src, lo, size, dev, row, e):
            act_on(remote(src.at[pl.ds(lo, size)], gbuf.at[pl.ds(in_window(dev, row), size)],
                          edge_send.at[e], edge_recv.at[e], dev), act)

        def up(src):
            go(src, 0, UP, me - 1, pick(me, NOMINAL), 0)

        def down(src):
            go(src, SHARE - DOWN, DOWN, me + 1, pick(me + 1, NOMINAL) - DOWN, 1)
        when_in(1, 1, up, ga)
        when_in(2, 2, up, gc)
        when_in(3, 5, up, gb)
        when_in(6, 7, up, gc)
        when_in(0, 1, down, ga)
        when_in(2, 4, down, gb)
        when_in(5, 6, down, gc)

    edges('start')
    share(ssl, ss_send, ss_recv, 'get')
    grad_sq = jnp.sum(sum(ssl[e] for e in range(N_DEV)))
    grad_sq = grad_sq * (1.0 / (N_DEV * N_DEV))
    norm = jnp.sqrt(jnp.full((8, LANES), grad_sq, F32))
    scale = (1.0 / N_DEV) / jnp.maximum(1.0, norm)
    scale = jnp.concatenate([scale] * (BLK // 8), axis=0)
    for e, (has, size) in enumerate(((me < N_DEV - 1, UP), (me > 0, DOWN))):
        @pl.when(has)
        def _():
            rows = gbuf.at[pl.ds(0, size)]
            remote(rows, rows, edge_send.at[e], edge_recv.at[e], sib).wait_recv()
    g_loads('wait')
    first_t, past_t = pick(me, FIRST_TENSOR), pick(me, PAST_TENSOR)

    def over(first, past, body):
        def tensor(t):
            lo = pick(t, STARTS[:-1]) - SHARD_ROWS * me
            hi = pick(t, STARTS[1:]) - SHARD_ROWS * me
            from_b = jnp.maximum(lo // BLK, first)
            to_b = jnp.maximum(from_b, jnp.minimum((hi + BLK - 1) // BLK, min(past, FULL)))

            def keep(b, size):
                ids = lax.broadcasted_iota(jnp.int32, (size, LANES), 0) + b * BLK
                return (ids >= lo) & (ids < hi)
            body(t, from_b, to_b, keep, past > FULL)
        each(first_t, past_t, tensor)

    REST = SHARD_ROWS - FULL * BLK

    def direction(t, first, past, keep_of, with_rest):
        decay = jnp.where((t % 2 == 0) & (t != 4) & (t < 9), DECAY, 0.0).astype(F32)

        def rows(at, g_at, keep, rate):
            g, w, m, v = gbuf[g_at, :], wbuf[at, :], mbuf[at, :], vbuf[at, :]
            h = g * rate
            new_m = BETA_ONE * m + (1.0 - BETA_ONE) * h
            new_v = BETA_TWO * v + (1.0 - BETA_TWO) * h * h
            u = (new_m * (1.0 / CORR_ONE)) / (jnp.sqrt(new_v * (1.0 / CORR_TWO)) + EPSILON) + decay * w
            mbuf[at, :] = jnp.where(keep, new_m, m)
            vbuf[at, :] = jnp.where(keep, new_v, v)
            gbuf[g_at, :] = jnp.where(keep, u, g)
            return jnp.where(keep, u * u, 0.0), jnp.where(keep, w * w, 0.0)

        def block(b, carry):
            found = rows(tile(b, BLK), pl.ds(pl.multiple_of(b * BLK + EDGE, DOWN), BLK), keep_of(b, BLK), scale)
            return tuple(total + jnp.sum(sq.reshape(-1, 8, LANES), axis=0) for total, sq in zip(carry, found))

        def note(at, sq):
            sums[me, pl.ds(at, 1), :] += jnp.sum(sq, axis=0, keepdims=True)
        zero = jnp.zeros((8, LANES), F32)
        found = lax.fori_loop(first, past, block, (zero, zero))
        note(t, found[0])
        note(DOWN + t, found[1])
        if with_rest:
            found = rows(pl.ds(FULL * BLK, REST), pl.ds(FULL * BLK + EDGE, REST), keep_of(FULL, REST), scale[:REST])
            note(t, found[0])
            note(DOWN + t, found[1])

    for k in range(LOADS):
        for c in loads[k]:
            c.wait()
        over(GB * k, GB * (k + 1) + (k == LOADS - 1), direction)
    share(sums, sum_send, sum_recv, 'start')
    share(sums, sum_send, sum_recv, 'get')
    total = jnp.sum(sum(sums[e] for e in range(N_DEV)), axis=1, keepdims=True)
    u_n, w_n = jnp.sqrt(total[:DOWN]), jnp.sqrt(total[DOWN:])
    both = (u_n > 0) & (w_n > 0)
    ratio = jnp.where(both, w_n / jnp.where(u_n > 0, u_n, 1.0), 1.0)
    rates[...] = jnp.broadcast_to(LEARN_RATE * ratio, rates.shape)

    def apply(t, first, past, keep_of, with_rest):
        def rows(at, g_at, keep):
            w = wbuf[at, :]
            rate = jnp.broadcast_to(rates[pl.ds(t, 1), :], w.shape)
            wbuf[at, :] = jnp.where(keep, w - rate * gbuf[g_at, :], w)

        def block(b):
            rows(tile(b, BLK), pl.ds(pl.multiple_of(b * BLK + EDGE, DOWN), BLK), keep_of(b, BLK))
        each(first, past, block)
        if with_rest:
            rows(pl.ds(FULL * BLK, REST), pl.ds(FULL * BLK + EDGE, REST), keep_of(FULL, REST))

    def cut(dev, j):
        return pl.ds(SHARD_ROWS * dev + CUTS[j], CUTS[j + 1] - CUTS[j])

    def twin(dev):
        return dev + other(2 * core)

    dg = N_DEV - 2 * (chip + 1) + core

    def own_part(j, e, sem, dev):
        return remote(wbuf.at[cut(0, j)], full.at[cut(me, j)], own_send.at[e, j], sem, dev)

    PB = SEG // BLK
    for j in range(PARTS):
        over(PB * j, PB * (j + 1) + (j == PARTS - 1), apply)
        for e, (sem, dev) in enumerate(((x_recv.at[j], xn), (y_recv.at[j], yn), (s_recv.at[0, j], sib))):
            own_part(j, e, sem, dev).start()
        local(wbuf.at[cut(0, j)], full.at[cut(me, j)], own_copy.at[j]).start()

    def wait_from(dev, j, sem):
        rows = full.at[cut(dev, j)]
        remote(rows, rows, cin_sem.at[0], sem, sib).wait_recv()

    def forward(dev, j, send_sem, recv_sem, to):
        rows = full.at[cut(dev, j)]
        remote(rows, rows, send_sem, recv_sem, to).start()

    def convert(*parts):
        todo = []
        for slot, (dev, j) in enumerate(parts):
            skip = DOWN if j == 0 else 0
            lo, size = pl.multiple_of(floor_of(dev) + skip + SEG * j, DOWN), SEG - skip
            cp = local(full.at[pl.ds(lo, size)], cin.at[slot, pl.ds(0, size)], cin_sem.at[slot])
            cp.start()
            todo.append((cp, slot, lo, size))
        for cp, slot, lo, size in todo:
            cp.wait()

            def body(b):
                params[pl.ds(pl.multiple_of(lo + b * DOWN, DOWN), DOWN), :] = cin[slot, tile(b, DOWN), :].astype(BF16)
            lax.fori_loop(0, size // DOWN, lambda b, c: (body(b), c)[1], 0, unroll=8)

    for j in range(PARTS):
        local(wbuf.at[cut(0, j)], full.at[cut(me, j)], own_copy.at[j]).wait()
        wait_from(sib, j, s_recv.at[0, j])
        convert((me, j), (sib, j))
        wait_from(xn, j, x_recv.at[j])
        forward(xn, j, sib_fwd.at[0, j], s_recv.at[1, j], sib)
        if j % 2 == 0:
            forward(xn, j, fwd_send.at[j], d_recv.at[j], yn)
        wait_from(yn, j, y_recv.at[j])
        forward(yn, j, sib_fwd.at[1, j], s_recv.at[2, j], sib)
        if j % 2 == 1:
            forward(yn, j, fwd_send.at[j], d_recv.at[j], xn)
        convert((xn, j), (yn, j))
        wait_from(twin(xn), j, s_recv.at[1, j])
        wait_from(twin(yn), j, s_recv.at[2, j])
        convert((twin(xn), j), (twin(yn), j))
    for j in range(0, PARTS, 2):
        both_parts = (j, j + 1)
        for e in both_parts:
            wait_from(dg, e, d_recv.at[e])
            forward(dg, e, sib_fwd.at[2, e], s_recv.at[3, e], sib)
        convert(*[(dg, e) for e in both_parts])
        for e in both_parts:
            wait_from(twin(dg), e, s_recv.at[3, e])
        if e == PARTS - 1:
            low = DOWN * (SHARD_ROWS * (N_DEV - 1) // DOWN) + SHARE
            pieces = ([(0, DOWN)] + [(DOWN * (SHARD_ROWS * s // DOWN) - DOWN, 2 * DOWN) for s in range(1, N_DEV)]
                      + [(low, TOTAL_ROWS - low)])
            ends = [local(full.at[pl.ds(lo, size)], cin.at[2, pl.ds(2 * DOWN * p, size)], cin_sem.at[2 + p])
                    for p, (lo, size) in enumerate(pieces)]
            for c in ends:
                c.start()
        convert(*[(twin(dg), e) for e in both_parts])
    for p, (c, (lo, size)) in enumerate(zip(ends, pieces)):
        c.wait()
        params[lo:lo + size, :] = cin[2, 2 * DOWN * p:2 * DOWN * p + size, :].astype(BF16)
    edges('sent')
    share(ssl, ss_send, ss_recv, 'sent')
    share(sums, sum_send, sum_recv, 'sent')
    for j in range(PARTS):
        sems = [fwd_send.at[j]] + [s.at[e, j] for s in (own_send, sib_fwd) for e in range(3)]
        for sem in sems:
            remote(wbuf.at[cut(0, j)], full.at[cut(me, j)], sem, x_recv.at[j], xn).wait_send()


def update_call(w, m, v, ga, gb, gc, vg, ss):
    shard = pltpu.VMEM((SHARD_ROWS, LANES), F32)
    outs = [shard, shard, shard, pltpu.VMEM((TOTAL_ROWS, LANES), BF16), shape(TOTAL_ROWS, LANES)]
    in_vmem = pl.BlockSpec(memory_space=pltpu.VMEM)
    return pl.pallas_call(
        update_kernel,
        out_shape=outs,
        in_specs=any_space(8),
        out_specs=[in_vmem] * 4 + any_space(1),
        scratch_shapes=[
            vmem(WIN, LANES), vmem(3, SEG, LANES),
            vmem(N_DEV, 8, LANES), vmem(N_DEV, 2 * DOWN, LANES), vmem(DOWN, LANES),
            *dmas((3, LOADS), 3, 2, 2, 7, N_DEV, 7, N_DEV, (3, PARTS), PARTS, PARTS, PARTS, PARTS, (4, PARTS),
                  PARTS, (3, PARTS), 11)],
        compiler_params=params_of(1, 14),
        name='lamb_gather',
    )(w, m, v, ga, gb, gc, vg, ss)


def write_kernel(*refs):
    *pairs, sem = refs
    half = len(pairs) // 2
    copies = [local(src, dst, sem.at[e]) for e, (src, dst) in enumerate(zip(pairs[:half], pairs[half:]))]
    for c in copies:
        c.start()
    for c in copies:
        c.wait()


def write_call(arrays):
    return pl.pallas_call(
        write_kernel,
        out_shape=[jax.ShapeDtypeStruct(a.shape, a.dtype) for a in arrays],
        in_specs=[pl.BlockSpec(memory_space=pltpu.VMEM)] * len(arrays),
        out_specs=any_space(len(arrays)),
        scratch_shapes=dmas(len(arrays)),
        compiler_params=pltpu.CompilerParams(vmem_limit_bytes=MIB),
        name='write_out',
    )(*arrays)


def solution(mesh):
    def local_step(weights, moment_one, moment_two, *rest):
        *acts, ln_grad = rest
        ga, gb, gc, vg, ss, *_ = reduce_call(acts, ln_grad[0])
        rows = [a.reshape(SHARD_ROWS, LANES) for a in (weights, moment_one, moment_two)]
        out = update_call(*rows, *(g.reshape(-1, LANES) for g in (ga, gb, gc, vg)), ss)
        return tuple(a.reshape(-1) for a in write_call(out[:-1]))

    row_spec = P('dp', None)
    flat_spec = P('dp')
    in_specs = (flat_spec,) * 3 + (row_spec,) * 8 + (P('dp', None, None),)
    return jax.shard_map(local_step, mesh=mesh, in_specs=in_specs, out_specs=(flat_spec,) * 3 + (P(),), check_vma=False)
```

time: 1360 us -> 481 us (0.35)
  waiting for transfers between devices: 798 us -> 0 us
  Pallas kernels: 0 us -> 478 us
  other arithmetic: 257 us -> 0 us
  matrix products: 128 us -> 0 us
  local copies, waits for them, and re-layouts: 104 us -> 0 us
  blocking collectives: 46.8 us -> 0 us
  between operations: 15.3 us -> 0.65 us
    unnamed x3 -> x0, waiting for transfers between devices: 570 us -> none
    pallas_call x0 -> x3, Pallas kernels: none -> 478 us  [the longest x1 238 us: update_call(): pl.pallas_call(update_kernel, out_shape=outs, in_specs=any_space(8), out_...]
    all_gather x1 -> x0, waiting for transfers between devices: 228 us -> none  [local_step(): lax.all_gather(new_w, 'dp', axis=0, tiled=True)]
    reduce_sum x7 -> x0, other arithmetic: 183 us -> none  [the longest x1 93.5 us: per_element(): jnp.sum(jnp.where(seg_ids[None, :] == seg_range, table[:, None], 0.0), ax...]
    dot_general x4 -> x0, matrix products: 128 us -> none  [weight_grad(): lax.dot_general(x_rows, dy_rows, CONTRACT_ROWS, preferred_element_type=jn...]
    unnamed x38 -> x0, local copies, waits for them, and re-layouts: 102 us -> none
    psum x2 -> x0, blocking collectives: 46.8 us -> none  [the longest x1 24.4 us: local_step(): total_sums = lax.psum(part_sums, 'dp')]
    convert_element_type x1 -> x0, other arithmetic: 25.4 us -> none  [local_step(): params = full_w.astype(jnp.bfloat16)]
  transfers between devices with their start and end apart: 2 -> 0, of which waited for: 2 -> 0; matrix products, arithmetic and copies ran while one was open for 0% -> 0% of each run, Pallas kernels for 0% -> 0%
where the time goes in v1:
time: 481 us; the launch traced here: 479 us
  Pallas kernels  478 us (99%)
    pallas_call x1, Pallas kernels, update_call(): pl.pallas_call(update_kernel, out_shape=outs, in_specs=any_space(8), out_...  238 us
    pallas_call x1, Pallas kernels, reduce_call(): pl.pallas_call(reduce_kernel, out_shape=outs, in_specs=any_space(len(acts...  226 us
    pallas_call x1, Pallas kernels, write_call(): pl.pallas_call(write_kernel, out_shape=[jax.ShapeDtypeStruct(a.shape, a.d...  14.8 us

profile of v1, /device:TPU:0, one launch (start us, length us, event | category | flops | bytes accessed | tf_op | source)
XLA Modules:
  0.0 479.0 jit_solution(13643836224488145931)
XLA Ops:
  0.6 225.7 %grad_reduce.1 = (f32[512,24,128]{2,1,0:T(8,128)}, f32[384,32,128]{2,1,0:T(8,128)}, f32[1536,8,128]{2,1,0:T(8,128)}, f32[8,8,128]{2,1,0:T(8,128)}, f32[8,128]{1,...) custom-call(bf16[4096,1024]{1,0:T(8,128)(2,1)} %xq.1, ...), custom_call_target="tpu_custom_call" | custom-call | tf_op jit(solution)/shard_map/grad_reduce/pallas_call | solution.py:427
  226.3 237.8 %lamb_gather.1 = (f32[12301,128]{1,0:T(8,128)S(1)}, f32[12301,128]{1,0:T(8,128)S(1)}, f32[12301,128]{1,0:T(8,128)S(1)}, bf16[98408,128]{1,0:T(8,128)(2,1)S(1)}, f32[98408,128]{1,0:T(8,128)}) custom-call(f32[12301,128]{1,0:T(8,128)} %bitcast.12, f32[12301,128]{1,0:T(8,128)} %bitcast.13, f32[12301,128]{1,0:T(8,128)} %bitcast.14, f32[12288,128]{1,0:T(8,128)} %bitcast.15, ...), custom_call_target="tpu_custom_call" | custom-call | tf_op jit(solution)/shard_map/lamb_gather/pallas_call | solution.py:703
  464.1 14.8 %write_out.1 = (f32[12301,128]{1,0:T(8,128)}, f32[12301,128]{1,0:T(8,128)}, f32[12301,128]{1,0:T(8,128)}, bf16[98408,128]{1,0:T(8,128)(2,1)}) custom-call(f32[12301,128]{1,0:T(8,128)S(1)} %get-tuple-element.22.refs_0_, f32[12301,128]{1,0:T(8,128)S(1)} %get-tuple-element.23.refs_1_, f32[12301,128]{1,0:T(8,128)S(1)} %get-tuple-element.24.refs_2_, ...), custom_call_target="tpu_custom_call" | custom-call | tf_op jit(solution)/shard_map/write_out/pallas_call | solution.py:729

commit v2 on v1

--- a/solution.py
+++ b/solution.py
@@ -305,11 +305,11 @@
                 total = lax.fori_loop(0, KC // LANES, add, jnp.zeros_like(ss))
                 vec[t, pl.ds(row, 1), :] += jnp.sum(total, axis=0, keepdims=True)
 
+            @pl.when((slot == 0) & (n > 0))
+            def _():
+                prefetch(n - 1)
+
             @pl.when((slot == 1) & (n > 0))
-            def _():
-                prefetch(n - 1)
-
-            @pl.when((slot == 2) & (n > 0))
             def _():
                 combine(n - 1)
                 send_own(n - 1)
@@ -423,7 +423,7 @@
 def reduce_call(acts, ln_rows):
     lands = UNITS + HALF
     outs = [shape(512, 24, LANES), shape(384, 32, LANES), shape(1536, 8, LANES), shape(8, 8, LANES), shape(8, LANES),
-            shape(4 * UNITS, UR, D), shape(lands, UR, D), shape(lands, UR, D)]
+            shape(CHUNKS * UNITS, UR, D), shape(lands, UR, D), shape(lands, UR, D)]
     return pl.pallas_call(
         reduce_kernel,
         out_shape=outs,
@@ -431,9 +431,9 @@
         out_specs=any_space(len(outs)),
         scratch_shapes=[
             vmem(CHUNKS, KC, BLOCK, dtype=BF16), vmem(CHUNKS, KC, D, dtype=BF16), vmem(3, BLOCK, D),
-            vmem(4 * UNITS, UR, D), vmem(4, UR, D), vmem(4, UR, D), vmem(2, UR, 8, LANES),
-            vmem(4, 8, D), vmem(4, 8, D), vmem(8, 8, LANES), vmem(7, 8, D), vmem(4, D), vmem(8, D), vmem(8, LANES),
-            *dmas(CHUNKS, CHUNKS, 4 * UNITS, 4 * UNITS, 3 * UNITS, lands, lands, 7, 7, 4, 4, 2, 2)],
+            vmem(CHUNKS * UNITS, UR, D), vmem(CHUNKS, UR, D), vmem(CHUNKS, UR, D), vmem(2, UR, 8, LANES),
+            vmem(CHUNKS, 8, D), vmem(CHUNKS, 8, D), vmem(8, 8, LANES), vmem(7, 8, D), vmem(CHUNKS, D), vmem(8, D), vmem(8, LANES),
+            *dmas(CHUNKS, CHUNKS, CHUNKS * UNITS, CHUNKS * UNITS, X1 * UNITS, lands, lands, 7, 7, CHUNKS, CHUNKS, 2, 2)],
         compiler_params=params_of(0, 62),
         name='grad_reduce',
     )(*acts, ln_rows)
@@ -442,9 +442,9 @@
 PARTS = 16
 SEG = SHARE // PARTS
 CUTS = [SEG * j for j in range(PARTS)] + [SHARD_ROWS]
-BLK = 64
+BLK = 128
 FULL = SHARE // BLK
-LOADS = 8
+LOADS = 4
 LOAD = SHARE // LOADS
 GB = FULL // LOADS
 
@@ -542,54 +542,71 @@
     g_loads('wait')
     first_t, past_t = pick(me, FIRST_TENSOR), pick(me, PAST_TENSOR)
 
-    def over(first, past, body):
+    REST = SHARD_ROWS - FULL * BLK
+
+    def over(first, past, whole, masked):
+        top = min(past, FULL)
+
         def tensor(t):
             lo = pick(t, STARTS[:-1]) - SHARD_ROWS * me
             hi = pick(t, STARTS[1:]) - SHARD_ROWS * me
-            from_b = jnp.maximum(lo // BLK, first)
-            to_b = jnp.maximum(from_b, jnp.minimum((hi + BLK - 1) // BLK, min(past, FULL)))
-
-            def keep(b, size):
+            head, tail = lo // BLK, hi // BLK
+            from_b = jnp.maximum((lo + BLK - 1) // BLK, first)
+            whole(t, from_b, jnp.maximum(from_b, jnp.minimum(tail, top)))
+
+            def shared(b, size, at, g_at):
                 ids = lax.broadcasted_iota(jnp.int32, (size, LANES), 0) + b * BLK
-                return (ids >= lo) & (ids < hi)
-            body(t, from_b, to_b, keep, past > FULL)
+                masked(t, at, g_at, (ids >= lo) & (ids < hi))
+
+            def end(e):
+                b = jnp.where(e == 0, head, tail)
+                cuts = jnp.where(e == 0, lo, hi) % BLK > 0
+                again = (e > 0) & (head == tail) & (lo % BLK > 0)
+
+                @pl.when(cuts & (b >= first) & (b < top) & jnp.logical_not(again))
+                def _():
+                    shared(b, BLK, *block_rows(b))
+            each(0, 2, end)
+            if past > FULL:
+                shared(FULL, REST, pl.ds(FULL * BLK, REST), pl.ds(FULL * BLK + EDGE, REST))
         each(first_t, past_t, tensor)
 
-    REST = SHARD_ROWS - FULL * BLK
-
-    def direction(t, first, past, keep_of, with_rest):
+    def block_rows(b):
+        return tile(b, BLK), pl.ds(pl.multiple_of(b * BLK + EDGE, DOWN), BLK)
+
+    def step_of(t, at, g_at):
         decay = jnp.where((t % 2 == 0) & (t != 4) & (t < 9), DECAY, 0.0).astype(F32)
-
-        def rows(at, g_at, keep, rate):
-            g, w, m, v = gbuf[g_at, :], wbuf[at, :], mbuf[at, :], vbuf[at, :]
-            h = g * rate
-            new_m = BETA_ONE * m + (1.0 - BETA_ONE) * h
-            new_v = BETA_TWO * v + (1.0 - BETA_TWO) * h * h
-            u = (new_m * (1.0 / CORR_ONE)) / (jnp.sqrt(new_v * (1.0 / CORR_TWO)) + EPSILON) + decay * w
-            mbuf[at, :] = jnp.where(keep, new_m, m)
-            vbuf[at, :] = jnp.where(keep, new_v, v)
-            gbuf[g_at, :] = jnp.where(keep, u, g)
-            return jnp.where(keep, u * u, 0.0), jnp.where(keep, w * w, 0.0)
-
+        g, w, m, v = gbuf[g_at, :], wbuf[at, :], mbuf[at, :], vbuf[at, :]
+        h = g * scale[:g.shape[0]]
+        new_m = BETA_ONE * m + (1.0 - BETA_ONE) * h
+        new_v = BETA_TWO * v + (1.0 - BETA_TWO) * (h * h)
+        root = new_v * lax.rsqrt(jnp.maximum(new_v, jnp.finfo(F32).tiny))
+        u = new_m / (root * (CORR_ONE / CORR_TWO ** 0.5) + EPSILON * CORR_ONE) + decay * w
+        return (g, w, m, v), (u, w, new_m, new_v)
+
+    def note(t, u_sq, w_sq):
+        sums[me, pl.ds(t, 1), :] += jnp.sum(u_sq, axis=0, keepdims=True)
+        sums[me, pl.ds(DOWN + t, 1), :] += jnp.sum(w_sq, axis=0, keepdims=True)
+
+    def direction(t, first, past):
         def block(b, carry):
-            found = rows(tile(b, BLK), pl.ds(pl.multiple_of(b * BLK + EDGE, DOWN), BLK), keep_of(b, BLK), scale)
-            return tuple(total + jnp.sum(sq.reshape(-1, 8, LANES), axis=0) for total, sq in zip(carry, found))
-
-        def note(at, sq):
-            sums[me, pl.ds(at, 1), :] += jnp.sum(sq, axis=0, keepdims=True)
+            at, g_at = block_rows(b)
+            _, (u, w, new_m, new_v) = step_of(t, at, g_at)
+            mbuf[at, :], vbuf[at, :], gbuf[g_at, :] = new_m, new_v, u
+            return tuple(total + jnp.sum((x * x).reshape(-1, 8, LANES), axis=0) for total, x in zip(carry, (u, w)))
         zero = jnp.zeros((8, LANES), F32)
-        found = lax.fori_loop(first, past, block, (zero, zero))
-        note(t, found[0])
-        note(DOWN + t, found[1])
-        if with_rest:
-            found = rows(pl.ds(FULL * BLK, REST), pl.ds(FULL * BLK + EDGE, REST), keep_of(FULL, REST), scale[:REST])
-            note(t, found[0])
-            note(DOWN + t, found[1])
+        note(t, *lax.fori_loop(first, past, block, (zero, zero)))
+
+    def direction_shared(t, at, g_at, keep):
+        (g, w, m, v), (u, _, new_m, new_v) = step_of(t, at, g_at)
+        mbuf[at, :], vbuf[at, :] = jnp.where(keep, new_m, m), jnp.where(keep, new_v, v)
+        gbuf[g_at, :] = jnp.where(keep, u, g)
+        note(t, jnp.where(keep, u * u, 0.0), jnp.where(keep, w * w, 0.0))
 
     for k in range(LOADS):
         for c in loads[k]:
             c.wait()
-        over(GB * k, GB * (k + 1) + (k == LOADS - 1), direction)
+        over(GB * k, GB * (k + 1) + (k == LOADS - 1), direction, direction_shared)
     share(sums, sum_send, sum_recv, 'start')
     share(sums, sum_send, sum_recv, 'get')
     total = jnp.sum(sum(sums[e] for e in range(N_DEV)), axis=1, keepdims=True)
@@ -598,17 +615,17 @@
     ratio = jnp.where(both, w_n / jnp.where(u_n > 0, u_n, 1.0), 1.0)
     rates[...] = jnp.broadcast_to(LEARN_RATE * ratio, rates.shape)
 
-    def apply(t, first, past, keep_of, with_rest):
-        def rows(at, g_at, keep):
-            w = wbuf[at, :]
-            rate = jnp.broadcast_to(rates[pl.ds(t, 1), :], w.shape)
-            wbuf[at, :] = jnp.where(keep, w - rate * gbuf[g_at, :], w)
+    def apply(t, first, past):
+        rate = jnp.broadcast_to(rates[pl.ds(t, 1), :], (BLK, LANES))
 
         def block(b):
-            rows(tile(b, BLK), pl.ds(pl.multiple_of(b * BLK + EDGE, DOWN), BLK), keep_of(b, BLK))
+            at, g_at = block_rows(b)
+            wbuf[at, :] = wbuf[at, :] - rate * gbuf[g_at, :]
         each(first, past, block)
-        if with_rest:
-            rows(pl.ds(FULL * BLK, REST), pl.ds(FULL * BLK + EDGE, REST), keep_of(FULL, REST))
+
+    def apply_shared(t, at, g_at, keep):
+        w = wbuf[at, :]
+        wbuf[at, :] = jnp.where(keep, w - jnp.broadcast_to(rates[pl.ds(t, 1), :], w.shape) * gbuf[g_at, :], w)
 
     def cut(dev, j):
         return pl.ds(SHARD_ROWS * dev + CUTS[j], CUTS[j + 1] - CUTS[j])
@@ -623,7 +640,7 @@
 
     PB = SEG // BLK
     for j in range(PARTS):
-        over(PB * j, PB * (j + 1) + (j == PARTS - 1), apply)
+        over(PB * j, PB * (j + 1) + (j == PARTS - 1), apply, apply_shared)
         for e, (sem, dev) in enumerate(((x_recv.at[j], xn), (y_recv.at[j], yn), (s_recv.at[0, j], sib))):
             own_part(j, e, sem, dev).start()
         local(wbuf.at[cut(0, j)], full.at[cut(me, j)], own_copy.at[j]).start()
@@ -715,10 +732,17 @@
     )(w, m, v, ga, gb, gc, vg, ss)
 
 
+def cuts_of(rows):
+    size, last = rows // CHUNKS // DOWN * DOWN, CHUNKS - 1
+    return [(size * e, size) for e in range(last)] + [(size * last, rows - size * last)]
+
+
 def write_kernel(*refs):
     *pairs, sem = refs
     half = len(pairs) // 2
-    copies = [local(src, dst, sem.at[e]) for e, (src, dst) in enumerate(zip(pairs[:half], pairs[half:]))]
+    copies = [local(src.at[pl.ds(lo, size)], dst.at[pl.ds(lo, size)], sem.at[p, e])
+              for p, (src, dst) in enumerate(zip(pairs[:half], pairs[half:]))
+              for e, (lo, size) in enumerate(cuts_of(src.shape[0]))]
     for c in copies:
         c.start()
     for c in copies:
@@ -731,7 +755,7 @@
         out_shape=[jax.ShapeDtypeStruct(a.shape, a.dtype) for a in arrays],
         in_specs=[pl.BlockSpec(memory_space=pltpu.VMEM)] * len(arrays),
         out_specs=any_space(len(arrays)),
-        scratch_shapes=dmas(len(arrays)),
+        scratch_shapes=dmas((len(arrays), CHUNKS)),
         compiler_params=pltpu.CompilerParams(vmem_limit_bytes=MIB),
         name='write_out',
     )(*arrays)

time: 481 us -> 480 us (level)
  no operation moved by 1% of the time
where the time goes in v2:
time: 480 us; the launch traced here: 478 us
  Pallas kernels  477 us (99%)
    pallas_call x1, Pallas kernels, update_call(): pl.pallas_call(update_kernel, out_shape=outs, in_specs=any_space(8), out_...  237 us
    pallas_call x1, Pallas kernels, reduce_call(): pl.pallas_call(reduce_kernel, out_shape=outs, in_specs=any_space(len(acts...  226 us
    pallas_call x1, Pallas kernels, write_call(): pl.pallas_call(write_kernel, out_shape=[jax.ShapeDtypeStruct(a.shape, a.d...  14.3 us

profile of v2, /device:TPU:0, one launch (start us, length us, event | category | flops | bytes accessed | tf_op | source)
XLA Modules:
  0.0 477.8 jit_solution(16498732077011111226)
XLA Ops:
  0.6 226.2 %grad_reduce.1 = (f32[512,24,128]{2,1,0:T(8,128)}, f32[384,32,128]{2,1,0:T(8,128)}, f32[1536,8,128]{2,1,0:T(8,128)}, f32[8,8,128]{2,1,0:T(8,128)}, f32[8,128]{1,...) custom-call(bf16[4096,1024]{1,0:T(8,128)(2,1)} %xq.1, ...), custom_call_target="tpu_custom_call" | custom-call | tf_op jit(solution)/shard_map/grad_reduce/pallas_call | solution.py:427
  226.8 236.6 %lamb_gather.1 = (f32[12301,128]{1,0:T(8,128)S(1)}, f32[12301,128]{1,0:T(8,128)S(1)}, f32[12301,128]{1,0:T(8,128)S(1)}, bf16[98408,128]{1,0:T(8,128)(2,1)S(1)}, f32[98408,128]{1,0:T(8,128)}) custom-call(f32[12301,128]{1,0:T(8,128)} %bitcast.12, f32[12301,128]{1,0:T(8,128)} %bitcast.13, f32[12301,128]{1,0:T(8,128)} %bitcast.14, f32[12288,128]{1,0:T(8,128)} %bitcast.15, ...), custom_call_target="tpu_custom_call" | custom-call | tf_op jit(solution)/shard_map/lamb_gather/pallas_call | solution.py:720
  463.4 14.3 %write_out.1 = (f32[12301,128]{1,0:T(8,128)}, f32[12301,128]{1,0:T(8,128)}, f32[12301,128]{1,0:T(8,128)}, bf16[98408,128]{1,0:T(8,128)(2,1)}) custom-call(f32[12301,128]{1,0:T(8,128)S(1)} %get-tuple-element.22.refs_0_, f32[12301,128]{1,0:T(8,128)S(1)} %get-tuple-element.23.refs_1_, f32[12301,128]{1,0:T(8,128)S(1)} %get-tuple-element.24.refs_2_, ...), custom_call_target="tpu_custom_call" | custom-call | tf_op jit(solution)/shard_map/write_out/pallas_call | solution.py:753

commit v3 on v2

--- a/solution.py
+++ b/solution.py
@@ -148,13 +148,13 @@
 
 def bias_of(q, i):
     square = is_square(i)
-    need = jnp.where(is_edge(q), jnp.where(q == 0, i % 2, i) == 0, jnp.where(q == 1, i == 1, ~square))
+    need = jnp.where(q == 0, i % 2 > 0, jnp.where(q == 1, i == CHUNKS, jnp.where(q == 2, ~square, i == HALF - 1)))
     return need, jnp.where(q == 0, i // 2, jnp.where(q == 2, pick(i, WIDE), 0))
 
 
 def reduce_kernel(xq, dyq, xp, dyp, xi, dyi, xo, dyo, ln,
                   g_a, g_b, g_c, v_out, ss_out, sib_land, x_land, y_land,
-                  xbuf, dybuf, acc, part, stage, stage_r, flat, vec, vsum, vflat, vland, lnbuf, ss, ss_small,
+                  xbuf, dybuf, acc, part, x_fin, y_fin, stage, stage_r, flat, vec, vsum, vflat, vland, lnbuf, ss, ss_small,
                   x_sem, dy_sem, sib_send, sib_recv, out_send, x_recv, y_recv,
                   v_send, v_recv, st_sem, sr_sem, fl_sem, misc_sem):
     me, chip, core, sib, xn, yn = neighbours()
@@ -232,35 +232,35 @@
 
             @pl.when(t == Y1)
             def _():
-                arrived(vland.at[4], v_recv.at[4])
+                arrived(vland.at[CHUNKS], v_recv.at[CHUNKS])
                 vsum[t] = vsum[t] + vland[4]
 
     def send_own(n):
         def body(t, u, s, e):
-            def go(land, recv, slot, dev):
-                remote(part.at[e], land.at[slot], out_send.at[e], recv.at[slot], dev).start()
+            def go(dst, recv, slot, dev):
+                remote(part.at[e], dst, out_send.at[e], recv.at[slot], dev).start()
 
             @pl.when((t == 0) & (u % 2 == 0))
             def _():
-                go(x_land, x_recv, u // 2, xn)
+                go(x_land.at[u // 2], x_recv, u // 2, xn)
 
             @pl.when((t == 0) & (u % 2 == 1))
             def _():
-                go(y_land, y_recv, u // 2, yn)
+                go(y_land.at[u // 2], y_recv, u // 2, yn)
 
             @pl.when(t == B1)
             def _():
-                go(x_land, x_recv, HALF + u, xn)
+                go(x_fin.at[u], x_recv, HALF + u, xn)
 
             @pl.when(t == Y1)
             def _():
-                go(y_land, y_recv, HALF + u, yn)
+                go(y_fin.at[u], y_recv, HALF + u, yn)
         own_units(n, core, body)
         t, i = task_of(n)
         for way, dev in enumerate((xn, xn, yn)):
             @pl.when((i == HALF - 1) & (t == way))
             def _():
-                remote(vsum.at[t], vland.at[4 + way], v_send.at[4 + way], v_recv.at[4 + way], dev).start()
+                remote(vsum.at[t], vland.at[CHUNKS + way], v_send.at[CHUNKS + way], v_recv.at[CHUNKS + way], dev).start()
 
     def sib_units(n, act):
         def body(t, u, s, e):
@@ -360,22 +360,17 @@
         local(flat.at[slot], g_c.at[tile(0, UR)], fl_sem.at[slot]).wait()
 
     def finish(u):
-        copies = []
-        for e, (land, recv) in enumerate(((x_land, x_recv), (y_land, y_recv))):
-            arrived(land.at[HALF + u], recv.at[HALF + u])
-            copies.append(local(land.at[HALF + u], stage.at[e], st_sem.at[e]))
-            copies[e].start()
         slot = u % 2
 
         @pl.when(u >= 2)
         def _():
             written(slot)
-        for c in copies:
-            c.wait()
+        arrived(x_fin.at[u], x_recv.at[HALF + u])
+        arrived(y_fin.at[u], y_recv.at[HALF + u])
 
         def add(r, total):
             rows = tile(r, 16)
-            val = part[here * UNITS + u, rows, :] + stage[0, rows, :] + stage[1, rows, :]
+            val = part[here * UNITS + u, rows, :] + x_fin[u, rows, :] + y_fin[u, rows, :]
             flat[slot, rows] = val.reshape(16, 8, LANES)
             return total + val[0:8] * val[0:8] + val[8:16] * val[8:16]
         ss[...] += lax.fori_loop(0, UR // 16, add, jnp.zeros_like(ss))
@@ -397,7 +392,7 @@
         c.wait()
     each(0, here * UNITS, lambda e: remote(part.at[e], x_land.at[0], out_send.at[e], x_recv.at[0], xn).wait_send())
     for way in range(3):
-        remote(vsum.at[way], vland.at[4], v_send.at[4 + way], v_recv.at[4], xn).wait_send()
+        remote(vsum.at[way], vland.at[CHUNKS], v_send.at[CHUNKS + way], v_recv.at[CHUNKS], xn).wait_send()
 
 
 def shape(*dims, dtype=F32):
@@ -423,7 +418,7 @@
 def reduce_call(acts, ln_rows):
     lands = UNITS + HALF
     outs = [shape(512, 24, LANES), shape(384, 32, LANES), shape(1536, 8, LANES), shape(8, 8, LANES), shape(8, LANES),
-            shape(CHUNKS * UNITS, UR, D), shape(lands, UR, D), shape(lands, UR, D)]
+            shape(CHUNKS * UNITS, UR, D), shape(HALF, UR, D), shape(HALF, UR, D)]
     return pl.pallas_call(
         reduce_kernel,
         out_shape=outs,
@@ -431,18 +426,20 @@
         out_specs=any_space(len(outs)),
         scratch_shapes=[
             vmem(CHUNKS, KC, BLOCK, dtype=BF16), vmem(CHUNKS, KC, D, dtype=BF16), vmem(3, BLOCK, D),
-            vmem(CHUNKS * UNITS, UR, D), vmem(CHUNKS, UR, D), vmem(CHUNKS, UR, D), vmem(2, UR, 8, LANES),
+            vmem(CHUNKS * UNITS, UR, D), vmem(UNITS, UR, D), vmem(UNITS, UR, D), vmem(CHUNKS, UR, D), vmem(CHUNKS, UR, D), vmem(2, UR, 8, LANES),
             vmem(CHUNKS, 8, D), vmem(CHUNKS, 8, D), vmem(8, 8, LANES), vmem(7, 8, D), vmem(CHUNKS, D), vmem(8, D), vmem(8, LANES),
             *dmas(CHUNKS, CHUNKS, CHUNKS * UNITS, CHUNKS * UNITS, X1 * UNITS, lands, lands, 7, 7, CHUNKS, CHUNKS, 2, 2)],
-        compiler_params=params_of(0, 62),
+        compiler_params=params_of(0, 63),
         name='grad_reduce',
     )(*acts, ln_rows)
 
 
-PARTS = 16
-SEG = SHARE // PARTS
-CUTS = [SEG * j for j in range(PARTS)] + [SHARD_ROWS]
 BLK = 128
+PART_BLOCKS = [7] * UNITS + [4, 4, 2, 2]
+PARTS = len(PART_BLOCKS)
+SEG = max(PART_BLOCKS) * BLK
+ENDS = [BLK * sum(PART_BLOCKS[:j]) for j in range(PARTS + 1)]
+CUTS = ENDS[:-1] + [SHARD_ROWS]
 FULL = SHARE // BLK
 LOADS = 4
 LOAD = SHARE // LOADS
@@ -496,9 +493,9 @@
         for c in group:
             c.start()
     sums[...] = jnp.zeros_like(sums)
-    ss_copy.wait()
     others = [lax.rem(me + e, N_DEV) for e in range(1, N_DEV)]
     enter(others)
+    ss_copy.wait()
 
     def share(buf, send, recv, act):
         for e, dev in enumerate(others):
@@ -638,9 +635,8 @@
     def own_part(j, e, sem, dev):
         return remote(wbuf.at[cut(0, j)], full.at[cut(me, j)], own_send.at[e, j], sem, dev)
 
-    PB = SEG // BLK
     for j in range(PARTS):
-        over(PB * j, PB * (j + 1) + (j == PARTS - 1), apply, apply_shared)
+        over(ENDS[j] // BLK, ENDS[j + 1] // BLK + (j == PARTS - 1), apply, apply_shared)
         for e, (sem, dev) in enumerate(((x_recv.at[j], xn), (y_recv.at[j], yn), (s_recv.at[0, j], sib))):
             own_part(j, e, sem, dev).start()
         local(wbuf.at[cut(0, j)], full.at[cut(me, j)], own_copy.at[j]).start()
@@ -657,7 +653,7 @@
         todo = []
         for slot, (dev, j) in enumerate(parts):
             skip = DOWN if j == 0 else 0
-            lo, size = pl.multiple_of(floor_of(dev) + skip + SEG * j, DOWN), SEG - skip
+            lo, size = pl.multiple_of(floor_of(dev) + skip + ENDS[j], DOWN), ENDS[j + 1] - ENDS[j] - skip
             cp = local(full.at[pl.ds(lo, size)], cin.at[slot, pl.ds(0, size)], cin_sem.at[slot])
             cp.start()
             todo.append((cp, slot, lo, size))

time: 480 us -> 473 us (0.985)
  Pallas kernels: 477 us -> 471 us
where the time goes in v3:
time: 473 us; the launch traced here: 472 us
  Pallas kernels  471 us (100%)
    pallas_call x1, Pallas kernels, update_call(): pl.pallas_call(update_kernel, out_shape=outs, in_specs=any_space(8), out_...  233 us
    pallas_call x1, Pallas kernels, reduce_call(): pl.pallas_call(reduce_kernel, out_shape=outs, in_specs=any_space(len(acts...  224 us
    pallas_call x1, Pallas kernels, write_call(): pl.pallas_call(write_kernel, out_shape=[jax.ShapeDtypeStruct(a.shape, a.d...  14.3 us

profile of v3, /device:TPU:0, one launch (start us, length us, event | category | flops | bytes accessed | tf_op | source)
XLA Modules:
  0.0 471.8 jit_solution(9775440692809135384)
XLA Ops:
  0.6 223.9 %grad_reduce.1 = (f32[512,24,128]{2,1,0:T(8,128)}, f32[384,32,128]{2,1,0:T(8,128)}, f32[1536,8,128]{2,1,0:T(8,128)}, f32[8,8,128]{2,1,0:T(8,128)}, f32[8,128]{1,...) custom-call(bf16[4096,1024]{1,0:T(8,128)(2,1)} %xq.1, ...), custom_call_target="tpu_custom_call" | custom-call | tf_op jit(solution)/shard_map/grad_reduce/pallas_call | solution.py:422
  224.5 232.9 %lamb_gather.1 = (f32[12301,128]{1,0:T(8,128)S(1)}, f32[12301,128]{1,0:T(8,128)S(1)}, f32[12301,128]{1,0:T(8,128)S(1)}, bf16[98408,128]{1,0:T(8,128)(2,1)S(1)}, f32[98408,128]{1,0:T(8,128)}) custom-call(f32[12301,128]{1,0:T(8,128)} %bitcast.12, f32[12301,128]{1,0:T(8,128)} %bitcast.13, f32[12301,128]{1,0:T(8,128)} %bitcast.14, f32[12288,128]{1,0:T(8,128)} %bitcast.15, ...), custom_call_target="tpu_custom_call" | custom-call | tf_op jit(solution)/shard_map/lamb_gather/pallas_call | solution.py:716
  457.5 14.3 %write_out.1 = (f32[12301,128]{1,0:T(8,128)}, f32[12301,128]{1,0:T(8,128)}, f32[12301,128]{1,0:T(8,128)}, bf16[98408,128]{1,0:T(8,128)(2,1)}) custom-call(f32[12301,128]{1,0:T(8,128)S(1)} %get-tuple-element.22.refs_0_, f32[12301,128]{1,0:T(8,128)S(1)} %get-tuple-element.23.refs_1_, f32[12301,128]{1,0:T(8,128)S(1)} %get-tuple-element.24.refs_2_, ...), custom_call_target="tpu_custom_call" | custom-call | tf_op jit(solution)/shard_map/write_out/pallas_call | solution.py:749

commit v4 on v3

--- a/solution.py
+++ b/solution.py
@@ -153,9 +153,9 @@
 
 
 def reduce_kernel(xq, dyq, xp, dyp, xi, dyi, xo, dyo, ln,
-                  g_a, g_b, g_c, v_out, ss_out, sib_land, x_land, y_land,
+                  g_a, g_b, g_c, v_out, ss_out, sib_land, relay,
                   xbuf, dybuf, acc, part, x_fin, y_fin, stage, stage_r, flat, vec, vsum, vflat, vland, lnbuf, ss, ss_small,
-                  x_sem, dy_sem, sib_send, sib_recv, out_send, x_recv, y_recv,
+                  x_sem, dy_sem, sib_send, sib_recv, out_send, relay_recv, x_recv, y_recv,
                   v_send, v_recv, st_sem, sr_sem, fl_sem, misc_sem):
     me, chip, core, sib, xn, yn = neighbours()
     kinds = ((xq, dyq), (xp, dyp), (xi, dyi), (xo, dyo))
@@ -178,7 +178,8 @@
         issue(jnp.int32(j))
     ln_copy = local(ln, lnbuf, misc_sem.at[0])
     ln_copy.start()
-    enter((sib, xn, yn))
+    x_base, y_base = xn - core, yn - core
+    enter((sib, xn, yn, x_base + other(core), y_base + other(core)))
     ln_copy.wait()
     ss[...] = jnp.zeros_like(ss)
     vec[...] = jnp.zeros_like(vec)
@@ -188,40 +189,48 @@
             def _():
                 vec[t, 1:3, :] = lnbuf[q - 1:q + 1, :]
 
-    def own_units(n, par, body):
+    def own_units(n, who, body):
         t, i = task_of(n)
-        s0, cnt, u0 = units_of(chip_of(t, chip), i, par)
-        each(s0, s0 + cnt, lambda s: body(t, u0 + s - s0, s, t * UNITS + u0 + s - s0))
-
-    def relayed(t, u, do):
-        @pl.when((t == B1) & (u % 2 == 1))
-        def _():
-            do(y_land, y_recv)
-
-        @pl.when((t == Y1) & (u % 2 == 0))
-        def _():
-            do(x_land, x_recv)
+        (s_a, _, u_a), (s_b, count_b, u_b) = [units_of(chip_of(t, chip), i, par) for par in range(2)]
+
+        def sub_block(s):
+            second = (s >= s_b) & (s < s_b + count_b)
+            par = jnp.where(second, 1, 0)
+            u = s + jnp.where(second, u_b - s_b, u_a - s_a)
+            pair = 2 * (u // 2) + par
+            owner = jnp.where(t == 0, u % 2, jnp.where(t == here, par, t - 1))
+            e = jnp.where(t == 0, pair, jnp.where(t == here, here * UNITS + u, UNITS + 2 * u + par))
+
+            @pl.when(owner == who)
+            def _():
+                body(t, par, u, s, e)
+        each(0, CHUNKS, sub_block)
+
+    def relayed(t, par, u, do):
+        @pl.when(((t == B1) & (u % 2 == 1)) | ((t == Y1) & (u % 2 == 0)))
+        def _():
+            do(2 * (u // 2) + par)
 
     def prefetch(n):
-        def body(t, u, s, e):
+        def body(t, par, u, s, e):
             arrived(sib_land.at[e], sib_recv.at[e])
             local(sib_land.at[e], stage.at[s], st_sem.at[s]).start()
 
-            def more(land, recv):
-                arrived(land.at[u // 2], recv.at[u // 2])
-                local(land.at[u // 2], stage_r.at[s], sr_sem.at[s]).start()
-            relayed(t, u, more)
+            def more(at):
+                arrived(relay.at[at], relay_recv.at[at])
+                local(relay.at[at], stage_r.at[s], sr_sem.at[s]).start()
+            relayed(t, par, u, more)
         own_units(n, core, body)
 
     def combine(n):
-        def body(t, u, s, e):
+        def body(t, par, u, s, e):
             local(sib_land.at[e], stage.at[s], st_sem.at[s]).wait()
             part[e] = acc[n % 3, tile(s, UR), :] + stage[s]
 
-            def more(land, recv):
-                local(land.at[u // 2], stage_r.at[s], sr_sem.at[s]).wait()
+            def more(at):
+                local(relay.at[at], stage_r.at[s], sr_sem.at[s]).wait()
                 part[e] = part[e] + stage_r[s]
-            relayed(t, u, more)
+            relayed(t, par, u, more)
         own_units(n, core, body)
         t, i = task_of(n)
 
@@ -233,28 +242,24 @@
             @pl.when(t == Y1)
             def _():
                 arrived(vland.at[CHUNKS], v_recv.at[CHUNKS])
-                vsum[t] = vsum[t] + vland[4]
+                vsum[t] = vsum[t] + vland[CHUNKS]
 
     def send_own(n):
-        def body(t, u, s, e):
+        def body(t, par, u, s, e):
             def go(dst, recv, slot, dev):
                 remote(part.at[e], dst, out_send.at[e], recv.at[slot], dev).start()
 
-            @pl.when((t == 0) & (u % 2 == 0))
-            def _():
-                go(x_land.at[u // 2], x_recv, u // 2, xn)
-
-            @pl.when((t == 0) & (u % 2 == 1))
-            def _():
-                go(y_land.at[u // 2], y_recv, u // 2, yn)
+            @pl.when(t == 0)
+            def _():
+                go(relay.at[e], relay_recv, e, jnp.where(core == 0, x_base + 1, y_base))
 
             @pl.when(t == B1)
             def _():
-                go(x_fin.at[u], x_recv, HALF + u, xn)
+                go(x_fin.at[u], x_recv, u, x_base + par)
 
             @pl.when(t == Y1)
             def _():
-                go(y_fin.at[u], y_recv, HALF + u, yn)
+                go(y_fin.at[u], y_recv, u, y_base + par)
         own_units(n, core, body)
         t, i = task_of(n)
         for way, dev in enumerate((xn, xn, yn)):
@@ -263,7 +268,7 @@
                 remote(vsum.at[t], vland.at[CHUNKS + way], v_send.at[CHUNKS + way], v_recv.at[CHUNKS + way], dev).start()
 
     def sib_units(n, act):
-        def body(t, u, s, e):
+        def body(t, par, u, s, e):
             act_on(remote(acc.at[n % 3, tile(s, UR)], sib_land.at[e], sib_send.at[e], sib_recv.at[e], sib), act)
         own_units(n, other(core), body)
 
@@ -365,8 +370,8 @@
         @pl.when(u >= 2)
         def _():
             written(slot)
-        arrived(x_fin.at[u], x_recv.at[HALF + u])
-        arrived(y_fin.at[u], y_recv.at[HALF + u])
+        arrived(x_fin.at[u], x_recv.at[u])
+        arrived(y_fin.at[u], y_recv.at[u])
 
         def add(r, total):
             rows = tile(r, 16)
@@ -390,7 +395,7 @@
     written(1)
     for c in tail:
         c.wait()
-    each(0, here * UNITS, lambda e: remote(part.at[e], x_land.at[0], out_send.at[e], x_recv.at[0], xn).wait_send())
+    each(0, here * UNITS, lambda e: remote(part.at[e], x_fin.at[0], out_send.at[e], x_recv.at[0], xn).wait_send())
     for way in range(3):
         remote(vsum.at[way], vland.at[CHUNKS], v_send.at[CHUNKS + way], v_recv.at[CHUNKS], xn).wait_send()
 
@@ -416,9 +421,8 @@
 
 
 def reduce_call(acts, ln_rows):
-    lands = UNITS + HALF
     outs = [shape(512, 24, LANES), shape(384, 32, LANES), shape(1536, 8, LANES), shape(8, 8, LANES), shape(8, LANES),
-            shape(CHUNKS * UNITS, UR, D), shape(HALF, UR, D), shape(HALF, UR, D)]
+            shape(CHUNKS * UNITS, UR, D), shape(UNITS, UR, D)]
     return pl.pallas_call(
         reduce_kernel,
         out_shape=outs,
@@ -428,7 +432,7 @@
             vmem(CHUNKS, KC, BLOCK, dtype=BF16), vmem(CHUNKS, KC, D, dtype=BF16), vmem(3, BLOCK, D),
             vmem(CHUNKS * UNITS, UR, D), vmem(UNITS, UR, D), vmem(UNITS, UR, D), vmem(CHUNKS, UR, D), vmem(CHUNKS, UR, D), vmem(2, UR, 8, LANES),
             vmem(CHUNKS, 8, D), vmem(CHUNKS, 8, D), vmem(8, 8, LANES), vmem(7, 8, D), vmem(CHUNKS, D), vmem(8, D), vmem(8, LANES),
-            *dmas(CHUNKS, CHUNKS, CHUNKS * UNITS, CHUNKS * UNITS, X1 * UNITS, lands, lands, 7, 7, CHUNKS, CHUNKS, 2, 2)],
+            *dmas(CHUNKS, CHUNKS, CHUNKS * UNITS, CHUNKS * UNITS, X1 * UNITS, UNITS, UNITS, UNITS, 7, 7, CHUNKS, CHUNKS, 2, 2)],
         compiler_params=params_of(0, 63),
         name='grad_reduce',
     )(*acts, ln_rows)
@@ -462,8 +466,9 @@
     def load_rows(k):
         return pl.ds(LOAD * k, LOAD if k < LOADS - 1 else SHARD_ROWS - LOAD * k)
 
+    order = [*range(1, LOADS - 1), 0, LOADS - 1]
     loads = [[local(src.at[load_rows(k)], dst.at[load_rows(k)], load_sem.at[e, k])
-              for e, (src, dst) in enumerate(((w_in, wbuf), (m_in, mbuf), (v_in, vbuf)))] for k in range(LOADS)]
+              for e, (src, dst) in enumerate(((w_in, wbuf), (m_in, mbuf), (v_in, vbuf)))] for k in order]
 
     def when_in(lo, hi, do, *args):
         @pl.when((me >= lo) & (me <= hi))
@@ -531,11 +536,6 @@
     norm = jnp.sqrt(jnp.full((8, LANES), grad_sq, F32))
     scale = (1.0 / N_DEV) / jnp.maximum(1.0, norm)
     scale = jnp.concatenate([scale] * (BLK // 8), axis=0)
-    for e, (has, size) in enumerate(((me < N_DEV - 1, UP), (me > 0, DOWN))):
-        @pl.when(has)
-        def _():
-            rows = gbuf.at[pl.ds(0, size)]
-            remote(rows, rows, edge_send.at[e], edge_recv.at[e], sib).wait_recv()
     g_loads('wait')
     first_t, past_t = pick(me, FIRST_TENSOR), pick(me, PAST_TENSOR)
 
@@ -600,8 +600,14 @@
         gbuf[g_at, :] = jnp.where(keep, u, g)
         note(t, jnp.where(keep, u * u, 0.0), jnp.where(keep, w * w, 0.0))
 
-    for k in range(LOADS):
-        for c in loads[k]:
+    for k, group in zip(order, loads):
+        if k == 0:
+            for e, (has, size) in enumerate(((me < N_DEV - 1, UP), (me > 0, DOWN))):
+                @pl.when(has)
+                def _():
+                    rows = gbuf.at[pl.ds(0, size)]
+                    remote(rows, rows, edge_send.at[e], edge_recv.at[e], sib).wait_recv()
+        for c in group:
             c.wait()
         over(GB * k, GB * (k + 1) + (k == LOADS - 1), direction, direction_shared)
     share(sums, sum_send, sum_recv, 'start')

time: 473 us -> 472 us (level)
  no operation moved by 1% of the time
where the time goes in v4:
time: 472 us; the launch traced here: 471 us
  Pallas kernels  470 us (100%)
    pallas_call x1, Pallas kernels, update_call(): pl.pallas_call(update_kernel, out_shape=outs, in_specs=any_space(8), out_...  231 us
    pallas_call x1, Pallas kernels, reduce_call(): pl.pallas_call(reduce_kernel, out_shape=outs, in_specs=any_space(len(acts...  225 us
    pallas_call x1, Pallas kernels, write_call(): pl.pallas_call(write_kernel, out_shape=[jax.ShapeDtypeStruct(a.shape, a.d...  14.3 us

profile of v4, /device:TPU:0, one launch (start us, length us, event | category | flops | bytes accessed | tf_op | source)
XLA Modules:
  0.0 470.8 jit_solution(4294250897239578784)
XLA Ops:
  0.6 224.6 %grad_reduce.1 = (f32[512,24,128]{2,1,0:T(8,128)}, f32[384,32,128]{2,1,0:T(8,128)}, f32[1536,8,128]{2,1,0:T(8,128)}, f32[8,8,128]{2,1,0:T(8,128)}, f32[8,128]{1,...) custom-call(bf16[4096,1024]{1,0:T(8,128)(2,1)} %xq.1, bf16[4096,3072]{1,0:T(8,128)(2,1)} %dyq.1, ...), custom_call_target="tpu_custom_call" | custom-call | tf_op jit(solution)/shard_map/grad_reduce/pallas_call | solution.py:426
  225.2 231.2 %lamb_gather.1 = (f32[12301,128]{1,0:T(8,128)S(1)}, f32[12301,128]{1,0:T(8,128)S(1)}, f32[12301,128]{1,0:T(8,128)S(1)}, bf16[98408,128]{1,0:T(8,128)(2,1)S(1)}, f32[98408,128]{1,0:T(8,128)}) custom-call(f32[12301,128]{1,0:T(8,128)} %bitcast.12, f32[12301,128]{1,0:T(8,128)} %bitcast.13, f32[12301,128]{1,0:T(8,128)} %bitcast.14, f32[12288,128]{1,0:T(8,128)} %bitcast.15, ...), custom_call_target="tpu_custom_call" | custom-call | tf_op jit(solution)/shard_map/lamb_gather/pallas_call | solution.py:722
  456.5 14.3 %write_out.1 = (f32[12301,128]{1,0:T(8,128)}, f32[12301,128]{1,0:T(8,128)}, f32[12301,128]{1,0:T(8,128)}, bf16[98408,128]{1,0:T(8,128)(2,1)}) custom-call(f32[12301,128]{1,0:T(8,128)S(1)} %get-tuple-element.22.refs_0_, f32[12301,128]{1,0:T(8,128)S(1)} %get-tuple-element.23.refs_1_, f32[12301,128]{1,0:T(8,128)S(1)} %get-tuple-element.24.refs_2_, ...), custom_call_target="tpu_custom_call" | custom-call | tf_op jit(solution)/shard_map/write_out/pallas_call | solution.py:755

commit v5 on v4

--- a/solution.py
+++ b/solution.py
@@ -18,6 +18,7 @@
 N_DEV = 8
 TOKENS = 4096
 LANES = 128
+SUB = 8
 SHARD_ROWS = 12301
 TOTAL_ROWS = N_DEV * SHARD_ROWS
 KC = 1024
@@ -195,7 +196,7 @@
 
         def sub_block(s):
             second = (s >= s_b) & (s < s_b + count_b)
-            par = jnp.where(second, 1, 0)
+            par = second.astype(jnp.int32)
             u = s + jnp.where(second, u_b - s_b, u_a - s_a)
             pair = 2 * (u // 2) + par
             owner = jnp.where(t == 0, u % 2, jnp.where(t == here, par, t - 1))
@@ -214,7 +215,10 @@
     def prefetch(n):
         def body(t, par, u, s, e):
             arrived(sib_land.at[e], sib_recv.at[e])
-            local(sib_land.at[e], stage.at[s], st_sem.at[s]).start()
+
+            @pl.when(n > 0)
+            def _():
+                local(sib_land.at[e], stage.at[s], st_sem.at[s]).start()
 
             def more(at):
                 arrived(relay.at[at], relay_recv.at[at])
@@ -224,7 +228,9 @@
 
     def combine(n):
         def body(t, par, u, s, e):
-            local(sib_land.at[e], stage.at[s], st_sem.at[s]).wait()
+            @pl.when(n > 0)
+            def _():
+                local(sib_land.at[e], stage.at[s], st_sem.at[s]).wait()
             part[e] = acc[n % 3, tile(s, UR), :] + stage[s]
 
             def more(at):
@@ -269,7 +275,10 @@
 
     def sib_units(n, act):
         def body(t, par, u, s, e):
-            act_on(remote(acc.at[n % 3, tile(s, UR)], sib_land.at[e], sib_send.at[e], sib_recv.at[e], sib), act)
+            for first, dst in ((True, stage.at[s]), (False, sib_land.at[e])):
+                @pl.when((n == 0) == first)
+                def _():
+                    act_on(remote(acc.at[n % 3, tile(s, UR)], dst, sib_send.at[e], sib_recv.at[e], sib), act)
         own_units(n, other(core), body)
 
     def task(n):
@@ -306,7 +315,7 @@
             def _():
                 def add(r, total):
                     block = dybuf[slot, tile(r, LANES), :].astype(F32)
-                    return total + jnp.sum(block.reshape(-1, 8, D), axis=0)
+                    return total + jnp.sum(block.reshape(-1, SUB, D), axis=0)
                 total = lax.fori_loop(0, KC // LANES, add, jnp.zeros_like(ss))
                 vec[t, pl.ds(row, 1), :] += jnp.sum(total, axis=0, keepdims=True)
 
@@ -314,7 +323,7 @@
             def _():
                 prefetch(n - 1)
 
-            @pl.when((slot == 1) & (n > 0))
+            @pl.when((slot == jnp.where(n == 1, 0, 1)) & (n > 0))
             def _():
                 combine(n - 1)
                 send_own(n - 1)
@@ -340,7 +349,7 @@
 
         @pl.when(chip == 0)
         def _():
-            go(g_a.at[tile(u % 4, UR), tile(u // 4, 8)])
+            go(g_a.at[tile(u % 4, UR), tile(u // 4, SUB)])
 
         @pl.when(chip == 3)
         def _():
@@ -351,7 +360,7 @@
 
         @pl.when(mid & few & (square < 0))
         def _():
-            go(g_b.at[tile(jnp.where(past, 0, 2), UR), tile(col, 8)])
+            go(g_b.at[tile(jnp.where(past, 0, 2), UR), tile(col, SUB)])
 
         @pl.when(mid & few & (square >= 0))
         def _():
@@ -359,7 +368,7 @@
 
         @pl.when(mid & jnp.logical_not(few))
         def _():
-            go(g_b.at[tile(u % 3, UR), tile(u // 3, 8)])
+            go(g_b.at[tile(u % 3, UR), tile(u // 3, SUB)])
 
     def written(slot):
         local(flat.at[slot], g_c.at[tile(0, UR)], fl_sem.at[slot]).wait()
@@ -376,7 +385,7 @@
         def add(r, total):
             rows = tile(r, 16)
             val = part[here * UNITS + u, rows, :] + x_fin[u, rows, :] + y_fin[u, rows, :]
-            flat[slot, rows] = val.reshape(16, 8, LANES)
+            flat[slot, rows] = val.reshape(16, SUB, LANES)
             return total + val[0:8] * val[0:8] + val[8:16] * val[8:16]
         ss[...] += lax.fori_loop(0, UR // 16, add, jnp.zeros_like(ss))
         write_unit(u, slot)
@@ -385,7 +394,7 @@
     arrived(vland.at[5], v_recv.at[5])
     arrived(vland.at[6], v_recv.at[6])
     val = vsum[here] + vland[5] + vland[6]
-    vflat[...] = val.reshape(8, 8, LANES)
+    vflat[...] = val.reshape(8, SUB, LANES)
     total = ss[...] + jnp.where(core == 0, 1.0, 0.0).astype(F32) * (val * val)
     ss_small[...] = sum(total[:, LANES * c:LANES * (c + 1)] for c in range(8))
     tail = [local(vflat, v_out, misc_sem.at[0]), local(ss_small, ss_out, misc_sem.at[1])]
@@ -421,7 +430,7 @@
 
 
 def reduce_call(acts, ln_rows):
-    outs = [shape(512, 24, LANES), shape(384, 32, LANES), shape(1536, 8, LANES), shape(8, 8, LANES), shape(8, LANES),
+    outs = [shape(512, 24, LANES), shape(384, 32, LANES), shape(1536, SUB, LANES), shape(8, SUB, LANES), shape(SUB, LANES),
             shape(CHUNKS * UNITS, UR, D), shape(UNITS, UR, D)]
     return pl.pallas_call(
         reduce_kernel,
@@ -430,8 +439,8 @@
         out_specs=any_space(len(outs)),
         scratch_shapes=[
             vmem(CHUNKS, KC, BLOCK, dtype=BF16), vmem(CHUNKS, KC, D, dtype=BF16), vmem(3, BLOCK, D),
-            vmem(CHUNKS * UNITS, UR, D), vmem(UNITS, UR, D), vmem(UNITS, UR, D), vmem(CHUNKS, UR, D), vmem(CHUNKS, UR, D), vmem(2, UR, 8, LANES),
-            vmem(CHUNKS, 8, D), vmem(CHUNKS, 8, D), vmem(8, 8, LANES), vmem(7, 8, D), vmem(CHUNKS, D), vmem(8, D), vmem(8, LANES),
+            vmem(CHUNKS * UNITS, UR, D), vmem(UNITS, UR, D), vmem(UNITS, UR, D), vmem(CHUNKS, UR, D), vmem(CHUNKS, UR, D), vmem(2, UR, SUB, LANES),
+            vmem(CHUNKS, 8, D), vmem(CHUNKS, 8, D), vmem(8, SUB, LANES), vmem(7, 8, D), vmem(CHUNKS, D), vmem(8, D), vmem(SUB, LANES),
             *dmas(CHUNKS, CHUNKS, CHUNKS * UNITS, CHUNKS * UNITS, X1 * UNITS, UNITS, UNITS, UNITS, 7, 7, CHUNKS, CHUNKS, 2, 2)],
         compiler_params=params_of(0, 63),
         name='grad_reduce',
@@ -533,7 +542,7 @@
     share(ssl, ss_send, ss_recv, 'get')
     grad_sq = jnp.sum(sum(ssl[e] for e in range(N_DEV)))
     grad_sq = grad_sq * (1.0 / (N_DEV * N_DEV))
-    norm = jnp.sqrt(jnp.full((8, LANES), grad_sq, F32))
+    norm = jnp.sqrt(jnp.full((SUB, LANES), grad_sq, F32))
     scale = (1.0 / N_DEV) / jnp.maximum(1.0, norm)
     scale = jnp.concatenate([scale] * (BLK // 8), axis=0)
     g_loads('wait')
@@ -590,8 +599,8 @@
             at, g_at = block_rows(b)
             _, (u, w, new_m, new_v) = step_of(t, at, g_at)
             mbuf[at, :], vbuf[at, :], gbuf[g_at, :] = new_m, new_v, u
-            return tuple(total + jnp.sum((x * x).reshape(-1, 8, LANES), axis=0) for total, x in zip(carry, (u, w)))
-        zero = jnp.zeros((8, LANES), F32)
+            return tuple(total + jnp.sum((x * x).reshape(-1, SUB, LANES), axis=0) for total, x in zip(carry, (u, w)))
+        zero = jnp.zeros((SUB, LANES), F32)
         note(t, *lax.fori_loop(first, past, block, (zero, zero)))
 
     def direction_shared(t, at, g_at, keep):
@@ -686,8 +695,18 @@
         wait_from(twin(xn), j, s_recv.at[1, j])
         wait_from(twin(yn), j, s_recv.at[2, j])
         convert((twin(xn), j), (twin(yn), j))
+    def drain(*sems):
+        for j, sem in enumerate(sems):
+            remote(wbuf.at[cut(0, j % PARTS)], full.at[cut(me, j % PARTS)], sem, x_recv.at[j % PARTS], xn).wait_send()
+
     for j in range(0, PARTS, 2):
         both_parts = (j, j + 1)
+        if both_parts[-1] == PARTS - 1:
+            edges('sent')
+            share(ssl, ss_send, ss_recv, 'sent')
+            share(sums, sum_send, sum_recv, 'sent')
+            for sems in ([own_send.at[e] for e in range(3)] + [sib_fwd.at[e] for e in range(2)]):
+                drain(*(sems.at[p] for p in range(PARTS)))
         for e in both_parts:
             wait_from(dg, e, d_recv.at[e])
             forward(dg, e, sib_fwd.at[2, e], s_recv.at[3, e], sib)
@@ -706,13 +725,8 @@
     for p, (c, (lo, size)) in enumerate(zip(ends, pieces)):
         c.wait()
         params[lo:lo + size, :] = cin[2, 2 * DOWN * p:2 * DOWN * p + size, :].astype(BF16)
-    edges('sent')
-    share(ssl, ss_send, ss_recv, 'sent')
-    share(sums, sum_send, sum_recv, 'sent')
-    for j in range(PARTS):
-        sems = [fwd_send.at[j]] + [s.at[e, j] for s in (own_send, sib_fwd) for e in range(3)]
-        for sem in sems:
-            remote(wbuf.at[cut(0, j)], full.at[cut(me, j)], sem, x_recv.at[j], xn).wait_send()
+    drain(*(fwd_send.at[j] for j in range(PARTS)))
+    drain(*(sib_fwd.at[2, j] for j in range(PARTS)))
 
 
 def update_call(w, m, v, ga, gb, gc, vg, ss):
@@ -726,7 +740,7 @@
         out_specs=[in_vmem] * 4 + any_space(1),
         scratch_shapes=[
             vmem(WIN, LANES), vmem(3, SEG, LANES),
-            vmem(N_DEV, 8, LANES), vmem(N_DEV, 2 * DOWN, LANES), vmem(DOWN, LANES),
+            vmem(N_DEV, SUB, LANES), vmem(N_DEV, 2 * DOWN, LANES), vmem(DOWN, LANES),
             *dmas((3, LOADS), 3, 2, 2, 7, N_DEV, 7, N_DEV, (3, PARTS), PARTS, PARTS, PARTS, PARTS, (4, PARTS),
                   PARTS, (3, PARTS), 11)],
         compiler_params=params_of(1, 14),

time: 472 us -> 472 us (level)
  no operation moved by 1% of the time
where the time goes in v5:
time: 472 us; the launch traced here: 471 us
  Pallas kernels  470 us (100%)
    pallas_call x1, Pallas kernels, update_call(): pl.pallas_call(update_kernel, out_shape=outs, in_specs=any_space(8), out_...  232 us
    pallas_call x1, Pallas kernels, reduce_call(): pl.pallas_call(reduce_kernel, out_shape=outs, in_specs=any_space(len(acts...  223 us
    pallas_call x1, Pallas kernels, write_call(): pl.pallas_call(write_kernel, out_shape=[jax.ShapeDtypeStruct(a.shape, a.d...  14.3 us

profile of v5, /device:TPU:0, one launch (start us, length us, event | category | flops | bytes accessed | tf_op | source)
XLA Modules:
  0.0 470.5 jit_solution(7066511734322728843)
XLA Ops:
  0.6 223.3 %grad_reduce.1 = (f32[512,24,128]{2,1,0:T(8,128)}, f32[384,32,128]{2,1,0:T(8,128)}, f32[1536,8,128]{2,1,0:T(8,128)}, f32[8,8,128]{2,1,0:T(8,128)}, f32[8,128]{1,...) custom-call(bf16[4096,1024]{1,0:T(8,128)(2,1)} %xq.1, bf16[4096,3072]{1,0:T(8,128)(2,1)} %dyq.1, ...), custom_call_target="tpu_custom_call" | custom-call | tf_op jit(solution)/shard_map/grad_reduce/pallas_call | solution.py:435
  223.9 232.3 %lamb_gather.1 = (f32[12301,128]{1,0:T(8,128)S(1)}, f32[12301,128]{1,0:T(8,128)S(1)}, f32[12301,128]{1,0:T(8,128)S(1)}, bf16[98408,128]{1,0:T(8,128)(2,1)S(1)}, f32[98408,128]{1,0:T(8,128)}) custom-call(f32[12301,128]{1,0:T(8,128)} %bitcast.12, f32[12301,128]{1,0:T(8,128)} %bitcast.13, f32[12301,128]{1,0:T(8,128)} %bitcast.14, f32[12288,128]{1,0:T(8,128)} %bitcast.15, ...), custom_call_target="tpu_custom_call" | custom-call | tf_op jit(solution)/shard_map/lamb_gather/pallas_call | solution.py:736
  456.2 14.3 %write_out.1 = (f32[12301,128]{1,0:T(8,128)}, f32[12301,128]{1,0:T(8,128)}, f32[12301,128]{1,0:T(8,128)}, bf16[98408,128]{1,0:T(8,128)(2,1)}) custom-call(f32[12301,128]{1,0:T(8,128)S(1)} %get-tuple-element.22.refs_0_, f32[12301,128]{1,0:T(8,128)S(1)} %get-tuple-element.23.refs_1_, f32[12301,128]{1,0:T(8,128)S(1)} %get-tuple-element.24.refs_2_, ...), custom_call_target="tpu_custom_call" | custom-call | tf_op jit(solution)/shard_map/write_out/pallas_call | solution.py:769

commit v6 on v5

--- a/solution.py
+++ b/solution.py
@@ -556,25 +556,28 @@
         def tensor(t):
             lo = pick(t, STARTS[:-1]) - SHARD_ROWS * me
             hi = pick(t, STARTS[1:]) - SHARD_ROWS * me
-            head, tail = lo // BLK, hi // BLK
-            from_b = jnp.maximum((lo + BLK - 1) // BLK, first)
-            whole(t, from_b, jnp.maximum(from_b, jnp.minimum(tail, top)))
-
-            def shared(b, size, at, g_at):
-                ids = lax.broadcasted_iota(jnp.int32, (size, LANES), 0) + b * BLK
-                masked(t, at, g_at, (ids >= lo) & (ids < hi))
-
-            def end(e):
-                b = jnp.where(e == 0, head, tail)
-                cuts = jnp.where(e == 0, lo, hi) % BLK > 0
-                again = (e > 0) & (head == tail) & (lo % BLK > 0)
-
-                @pl.when(cuts & (b >= first) & (b < top) & jnp.logical_not(again))
-                def _():
-                    shared(b, BLK, *block_rows(b))
-            each(0, 2, end)
-            if past > FULL:
-                shared(FULL, REST, pl.ds(FULL * BLK, REST), pl.ds(FULL * BLK + EDGE, REST))
+
+            @pl.when((hi > first * BLK) & (lo < past * BLK))
+            def _():
+                head, tail = lo // BLK, hi // BLK
+                from_b = jnp.maximum((lo + BLK - 1) // BLK, first)
+                whole(t, from_b, jnp.maximum(from_b, jnp.minimum(tail, top)))
+
+                def shared(b, size, at, g_at):
+                    ids = lax.broadcasted_iota(jnp.int32, (size, LANES), 0) + b * BLK
+                    masked(t, at, g_at, (ids >= lo) & (ids < hi))
+
+                def end(e):
+                    b = jnp.where(e == 0, head, tail)
+                    cuts = jnp.where(e == 0, lo, hi) % BLK > 0
+                    again = (e > 0) & (head == tail) & (lo % BLK > 0)
+
+                    @pl.when(cuts & (b >= first) & (b < top) & jnp.logical_not(again))
+                    def _():
+                        shared(b, BLK, *block_rows(b))
+                each(0, 2, end)
+                if past > FULL:
+                    shared(FULL, REST, pl.ds(FULL * BLK, REST), pl.ds(FULL * BLK + EDGE, REST))
         each(first_t, past_t, tensor)
 
     def block_rows(b):
@@ -695,9 +698,9 @@
         wait_from(twin(xn), j, s_recv.at[1, j])
         wait_from(twin(yn), j, s_recv.at[2, j])
         convert((twin(xn), j), (twin(yn), j))
-    def drain(*sems):
-        for j, sem in enumerate(sems):
-            remote(wbuf.at[cut(0, j % PARTS)], full.at[cut(me, j % PARTS)], sem, x_recv.at[j % PARTS], xn).wait_send()
+    def drain(sems, parts):
+        for p in parts:
+            remote(wbuf.at[cut(0, p)], full.at[cut(me, p)], sems.at[p], x_recv.at[p], xn).wait_send()
 
     for j in range(0, PARTS, 2):
         both_parts = (j, j + 1)
@@ -706,7 +709,9 @@
             share(ssl, ss_send, ss_recv, 'sent')
             share(sums, sum_send, sum_recv, 'sent')
             for sems in ([own_send.at[e] for e in range(3)] + [sib_fwd.at[e] for e in range(2)]):
-                drain(*(sems.at[p] for p in range(PARTS)))
+                drain(sems, range(PARTS))
+            for sems in (fwd_send, sib_fwd.at[2]):
+                drain(sems, range(j))
         for e in both_parts:
             wait_from(dg, e, d_recv.at[e])
             forward(dg, e, sib_fwd.at[2, e], s_recv.at[3, e], sib)
@@ -725,8 +730,8 @@
     for p, (c, (lo, size)) in enumerate(zip(ends, pieces)):
         c.wait()
         params[lo:lo + size, :] = cin[2, 2 * DOWN * p:2 * DOWN * p + size, :].astype(BF16)
-    drain(*(fwd_send.at[j] for j in range(PARTS)))
-    drain(*(sib_fwd.at[2, j] for j in range(PARTS)))
+    for sems in (fwd_send, sib_fwd.at[2]):
+        drain(sems, both_parts)
 
 
 def update_call(w, m, v, ga, gb, gc, vg, ss):

time: 472 us -> 471 us (level)
  no operation moved by 1% of the time
where the time goes in v6:
time: 471 us; the launch traced here: 470 us
  Pallas kernels  469 us (100%)
    pallas_call x1, Pallas kernels, update_call(): pl.pallas_call(update_kernel, out_shape=outs, in_specs=any_space(8), out_...  232 us
    pallas_call x1, Pallas kernels, reduce_call(): pl.pallas_call(reduce_kernel, out_shape=outs, in_specs=any_space(len(acts...  223 us
    pallas_call x1, Pallas kernels, write_call(): pl.pallas_call(write_kernel, out_shape=[jax.ShapeDtypeStruct(a.shape, a.d...  14.3 us

profile of v6, /device:TPU:0, one launch (start us, length us, event | category | flops | bytes accessed | tf_op | source)
XLA Modules:
  0.0 469.8 jit_solution(3055460023022006567)
XLA Ops:
  0.6 223.3 %grad_reduce.1 = (f32[512,24,128]{2,1,0:T(8,128)}, f32[384,32,128]{2,1,0:T(8,128)}, f32[1536,8,128]{2,1,0:T(8,128)}, f32[8,8,128]{2,1,0:T(8,128)}, f32[8,128]{1,...) custom-call(bf16[4096,1024]{1,0:T(8,128)(2,1)} %xq.1, bf16[4096,3072]{1,0:T(8,128)(2,1)} %dyq.1, ...), custom_call_target="tpu_custom_call" | custom-call | tf_op jit(solution)/shard_map/grad_reduce/pallas_call | solution.py:435
  223.9 231.5 %lamb_gather.1 = (f32[12301,128]{1,0:T(8,128)S(1)}, f32[12301,128]{1,0:T(8,128)S(1)}, f32[12301,128]{1,0:T(8,128)S(1)}, bf16[98408,128]{1,0:T(8,128)(2,1)S(1)}, f32[98408,128]{1,0:T(8,128)}) custom-call(f32[12301,128]{1,0:T(8,128)} %bitcast.12, f32[12301,128]{1,0:T(8,128)} %bitcast.13, f32[12301,128]{1,0:T(8,128)} %bitcast.14, f32[12288,128]{1,0:T(8,128)} %bitcast.15, ...), custom_call_target="tpu_custom_call" | custom-call | tf_op jit(solution)/shard_map/lamb_gather/pallas_call | solution.py:741
  455.4 14.3 %write_out.1 = (f32[12301,128]{1,0:T(8,128)}, f32[12301,128]{1,0:T(8,128)}, f32[12301,128]{1,0:T(8,128)}, bf16[98408,128]{1,0:T(8,128)(2,1)}) custom-call(f32[12301,128]{1,0:T(8,128)S(1)} %get-tuple-element.22.refs_0_, f32[12301,128]{1,0:T(8,128)S(1)} %get-tuple-element.23.refs_1_, f32[12301,128]{1,0:T(8,128)S(1)} %get-tuple-element.24.refs_2_, ...), custom_call_target="tpu_custom_call" | custom-call | tf_op jit(solution)/shard_map/write_out/pallas_call | solution.py:774
